TPU v7x, 256 devices: a 2x2x32 block of a 4x8x32 slice. The times are simulated.
256 devices in a mesh: members: 4 (over y, x), zonal: 32 (over z), merid: 2 (over core).
Axes of the slice: x: 2, y: 2, z: 32, core: 2. Of those that a mesh axis runs over, the one named last changes fastest.
The devices are a block of a 4x8x32 slice.
Arguments:
- height: float32 [2048, 1024], P(('members', 'zonal'), 'merid'), parts along dimension 0, may hold values from -6 to 6
- transport_u: float32 [2048, 1024], P(('members', 'zonal'), 'merid'), parts along dimension 0, may hold values from -4 to 4
- transport_v: float32 [2048, 1024], P(('members', 'zonal'), 'merid'), parts along dimension 0, may hold values from -4 to 4
- thickness: float32 [14, 2048, 1024], P(None, ('members', 'zonal'), 'merid'), parts along dimension 1, may hold values from 0.5 to 2
- velocity_u: float32 [14, 2048, 1024], P(None, ('members', 'zonal'), 'merid'), parts along dimension 1, may hold values from -3 to 3
- velocity_v: float32 [14, 2048, 1024], P(None, ('members', 'zonal'), 'merid'), parts along dimension 1, may hold values from -3 to 3
- sea_faces: int32 [2, 512, 1024], P(None, 'zonal', 'merid'), may hold values 0 or 1
- wind_seeds: int32 [16, 2], P('members'), parts along dimension 0, may hold values from 1 to 96
- wind_scale: float32 [16], P('members'), parts along dimension 0, may hold values from 0.5 to 2
- wind_base: float32 [2, 512, 1024], P(None, 'zonal', 'merid'), may hold values from -6 to 6
Outputs:
- final_height: float32 [2048, 1024], P(('members', 'zonal'), 'merid'), parts along dimension 0
- final_transport_u: float32 [2048, 1024], P(('members', 'zonal'), 'merid'), parts along dimension 0
- final_transport_v: float32 [2048, 1024], P(('members', 'zonal'), 'merid'), parts along dimension 0
- final_thickness: float32 [14, 2048, 1024], P(None, ('members', 'zonal'), 'merid'), parts along dimension 1
- final_velocity_u: float32 [14, 2048, 1024], P(None, ('members', 'zonal'), 'merid'), parts along dimension 1
- final_velocity_v: float32 [14, 2048, 1024], P(None, ('members', 'zonal'), 'merid'), parts along dimension 1
There are 4 independent parts, one for each index of `members`. A program takes and returns all parts, laid end to end along the dimension named above; an argument that names none is the same for every part. Nothing has to cross between parts.
All inputs are finite; a program needn't handle non-finite values. No bound on the sum of `sea_faces` on one device may be relied on, other than what follows from the above.
Results may differ from a plain program's by a relative error of at most 0.0001.
Values sent between devices are 32-bit elements; how exact they have to be, the bound alone decides.
A program may use at most 64 MiB of HBM per device.

v0:
```python
import math

import jax
import jax.numpy as jnp
from jax import lax
from jax.sharding import PartitionSpec as P

NSUB = 6
STEPS = 2


WAVE_LIMIT = 0.225
STRESS_SCALE = 0.1
FLUX_STEP = 0.05
PRESS_COEF = 0.05


def sent_to_all(value, axis):
    copies = jnp.broadcast_to(value, (lax.axis_size(axis), *value.shape))
    return lax.all_to_all(copies, axis, split_axis=0, concat_axis=0, tiled=True)


def in_order(pieces, dim):
    pieces = jnp.moveaxis(pieces, 0, dim)
    dims = pieces.shape
    return pieces.reshape(*dims[:dim], dims[dim] * dims[dim + 1], *dims[dim + 2 :])


def collect(value, axis, dim):
    pieces = sent_to_all(value, axis)
    return in_order(pieces, dim)


def extended(value, sides, width):
    for axis, dim in sides:
        devices, length = (lax.axis_size(axis), value.shape[dim])
        up = [(i, (i + 1) % devices) for i in range(devices)]
        down = [(j, i) for i, j in up]
        last = lax.slice_in_dim(value, length - width, length, axis=dim)
        leading = lax.slice_in_dim(value, 0, width, axis=dim)
        before = lax.ppermute(last, axis, up)
        after = lax.ppermute(leading, axis, down)
        value = jnp.concatenate([before, value, after], axis=dim)
    return value


def padded_2(value, sides, width):
    edges = {}
    for axis, dim in sides:
        devices, length = (lax.axis_size(axis), value.shape[dim])
        up = [(i, (i + 1) % devices) for i in range(devices)]
        last = lax.slice_in_dim(value, length - width, length, axis=dim)
        leading = lax.slice_in_dim(value, 0, width, axis=dim)
        edges[dim] = (
            lax.ppermute(last, axis, up),
            lax.ppermute(leading, axis, [(b, a) for a, b in up]),
        )
    done = []
    for _, dim in sides:
        low, high = edges[dim]
        around = [(width, width) if d in done else (0, 0) for d in range(value.ndim)]
        value = jnp.concatenate([jnp.pad(low, around), value, jnp.pad(high, around)], axis=dim)
        done.append(dim)
    return value


def from_behind(block, axis, distance):
    devices = range(lax.axis_size(axis))
    route = [((i - distance) % len(devices), i) for i in devices]
    return lax.ppermute(block, axis, route)


def shifted(block, axis, distance):
    devices = range(lax.axis_size(axis))
    route = [(i - distance, i) for i in devices if i - distance in devices]
    return lax.ppermute(block, axis, route)


def perturb(columns, rows_idx, wind_seeds, wind_scale, total_x, total_y):
    wave_x = wind_seeds[:, 0]
    wave_y = wind_seeds[:, 1]
    phase = (wave_x[:, None, None] * columns[None, :, None] % total_x).astype(jnp.float32) / total_x
    phase = (
        phase
        + (wave_y[:, None, None] * rows_idx[None, None, :] % total_y).astype(jnp.float32) / total_y
    )
    angle = 2.0 * math.pi * phase
    amplitude = wind_scale[:, None, None]
    return (
        jnp.sum(amplitude * jnp.cos(angle), axis=0),
        jnp.sum(amplitude * jnp.sin(angle), axis=0),
    )


def mirror_layers(top_rows):
    zonal_cells = top_rows.shape[1]
    whole = lax.all_gather(top_rows, "zonal", axis=1, tiled=True)
    start = (lax.axis_size("zonal") - 1 - lax.axis_index("zonal")) * zonal_cells
    piece = lax.dynamic_slice_in_dim(whole, start, zonal_cells, 1)
    return jnp.flip(piece, 1)


def mirror_static(block):
    width = block.shape[1]
    whole = collect(block, "zonal", 1)
    start = (lax.axis_size("zonal") - 1 - lax.axis_index("zonal")) * width
    piece = lax.dynamic_slice_in_dim(whole, start, width, 1)
    return piece


def mirror_state(block):
    width = block.shape[1]
    whole = collect(block, "zonal", 1)
    start = (lax.axis_size("zonal") - 1 - lax.axis_index("zonal")) * width
    piece = lax.dynamic_slice_in_dim(whole, start, width, 1)
    return piece


def clear_below(padded, merid_cells, margin):
    rows_ext = (
        lax.axis_index("merid") * merid_cells
        - margin
        + lax.broadcasted_iota(jnp.int32, (1, 1, padded.shape[2]), 2)
    )
    return jnp.where(rows_ext < 0, jnp.float32(0.0), padded)


def put_fold(north_field, folded, top):
    merid_cells = north_field.shape[-1]
    last = (
        lax.broadcasted_iota(jnp.int32, north_field.shape, north_field.ndim - 1) == merid_cells - 1
    )
    return jnp.where(jnp.logical_and(top, last), folded[..., None], north_field)


def from_low(field, axis):
    length = field.shape[axis]
    zero = jnp.zeros_like(lax.slice_in_dim(field, 0, 1, axis=axis))
    return jnp.concatenate([zero, lax.slice_in_dim(field, 0, length - 1, axis=axis)], axis=axis)


def from_high(field, axis):
    length = field.shape[axis]
    zero = jnp.zeros_like(lax.slice_in_dim(field, 0, 1, axis=axis))
    return jnp.concatenate([lax.slice_in_dim(field, 1, length, axis=axis), zero], axis=axis)


def advance_height(state):
    surface, flow_u, flow_v = state
    return surface - (flow_u - from_low(flow_u, 0) + flow_v - from_low(flow_v, 1))


def update_flows(surface, north_surf, state, statics):
    mask_u, mask_v, wave, stress_x, stress_y = statics
    flow_u = mask_u * (state[1] - wave * (from_high(surface, 0) - surface) + stress_x)
    flow_v = mask_v * (state[2] - wave * (north_surf - surface) + stress_y)
    return (surface, flow_u, flow_v)


def prepare_wide(mask_u, mask_v, wave, wind_base, wind_seeds, wind_scale, total_x, total_y):
    zonal_cells, merid_cells = wave.shape
    margin = NSUB + 1
    packed = jnp.stack([mask_u, mask_v, wave, wind_base[0], wind_base[1]])
    padded = extended(packed, (("zonal", 1), ("merid", 2)), margin)
    padded = clear_below(padded, merid_cells, margin)
    far = mirror_static(padded[:, :, merid_cells : merid_cells + margin])
    width = zonal_cells + 2 * margin
    spots = jnp.arange(width, dtype=jnp.int32)
    cols_own = (lax.axis_index("zonal") * zonal_cells - margin + spots) % total_x
    cols_far = (
        (lax.axis_size("zonal") - 1 - lax.axis_index("zonal")) * zonal_cells - margin + spots
    ) % total_x
    rows_own = (
        lax.axis_index("merid") * merid_cells
        - margin
        + jnp.arange(merid_cells + 2 * margin, dtype=jnp.int32)
    )
    rows_far = total_y - margin + jnp.arange(margin, dtype=jnp.int32)
    own_cos, own_sin = perturb(cols_own, rows_own, wind_seeds, wind_scale, total_x, total_y)
    far_cos, far_sin = perturb(cols_far, rows_far, wind_seeds, wind_scale, total_x, total_y)
    own = (
        padded[0],
        padded[1],
        padded[2],
        STRESS_SCALE * (padded[3] + own_cos),
        STRESS_SCALE * (padded[4] + own_sin),
    )
    mirrored = (
        far[0],
        far[1],
        far[2],
        STRESS_SCALE * (far[3] + far_cos),
        STRESS_SCALE * (far[4] + far_sin),
    )
    return (own, mirrored)


def interior(field, margin, zonal_cells, merid_cells):
    return field[margin : margin + zonal_cells, margin : margin + merid_cells]


def wide_substeps(surface, flow_u, flow_v, own, mirrored, top):
    zonal_cells, merid_cells = surface.shape
    margin = NSUB + 1
    packed = jnp.stack([surface, flow_u, flow_v])
    padded = extended(packed, (("zonal", 1), ("merid", 2)), margin)
    padded = clear_below(padded, merid_cells, margin)
    far = mirror_state(padded[:, :, merid_cells : merid_cells + margin])
    top_row = margin + merid_cells - 1
    row_ids = lax.broadcasted_iota(jnp.int32, padded.shape[1:], 1)
    fold_here = jnp.logical_and(top, row_ids == top_row)
    far_top = lax.broadcasted_iota(jnp.int32, far.shape[1:], 1) == margin - 1
    own_state = (padded[0], padded[1], padded[2])
    far_state = (far[0], far[1], far[2])
    sum_u = jnp.zeros_like(padded[1])
    sum_v = jnp.zeros_like(padded[2])
    for inner in range(NSUB):
        own_eta = advance_height(own_state)
        far_eta = advance_height(far_state)
        own_north = jnp.where(
            fold_here, jnp.flip(far_eta[:, margin - 1], 0)[:, None], from_high(own_eta, 1)
        )
        far_north = jnp.where(
            far_top, jnp.flip(own_eta[:, top_row], 0)[:, None], from_high(far_eta, 1)
        )
        own_state = update_flows(own_eta, own_north, own_state, own)
        far_state = update_flows(far_eta, far_north, far_state, mirrored)
        sum_u = sum_u + own_state[1]
        sum_v = sum_v + own_state[2]
    surface = interior(own_state[0], margin, zonal_cells, merid_cells)
    flow_u = interior(own_state[1], margin, zonal_cells, merid_cells)
    flow_v = interior(own_state[2], margin, zonal_cells, merid_cells)
    mean_u = interior(sum_u, margin, zonal_cells, merid_cells) / NSUB
    mean_v = interior(sum_v, margin, zonal_cells, merid_cells) / NSUB
    return (surface, flow_u, flow_v, mean_u, mean_v)


def layer_neighbours(thick, speed_u, speed_v, top):
    layers, zonal_cells, merid_cells = thick.shape
    folded = mirror_layers(thick[:, :, merid_cells - 1])
    thick_pad = padded_2(thick, (("zonal", 1), ("merid", 2)), 1)
    west_column = from_behind(speed_u[:, zonal_cells - 1 :, :], "zonal", 1)
    west_u = jnp.concatenate([west_column, speed_u[:, : zonal_cells - 1, :]], axis=1)
    south_row = shifted(speed_v[:, :, merid_cells - 1 :], "merid", 1)
    south_v = jnp.concatenate([south_row, speed_v[:, :, : merid_cells - 1]], axis=2)
    east_h = thick_pad[:, 2:, 1 : merid_cells + 1]
    west_h = thick_pad[:, :zonal_cells, 1 : merid_cells + 1]
    south_h = thick_pad[:, 1 : zonal_cells + 1, :merid_cells]
    north_h = put_fold(thick_pad[:, 1 : zonal_cells + 1, 2:], folded, top)
    return (east_h, west_h, south_h, north_h, west_u, south_v)


def body(
    height,
    transport_u,
    transport_v,
    thickness,
    velocity_u,
    velocity_v,
    sea_faces,
    wind_seeds,
    wind_scale,
    wind_base,
):
    zonal_cells, merid_cells = height.shape
    total_x = zonal_cells * lax.axis_size("zonal")
    total_y = merid_cells * lax.axis_size("merid")
    top = lax.axis_index("merid") == lax.axis_size("merid") - 1
    mask_u = sea_faces[0].astype(jnp.float32)
    mask_v = sea_faces[1].astype(jnp.float32)
    layers = thickness.shape[0]
    wave = WAVE_LIMIT / layers * jnp.sum(thickness, axis=0)
    own_static, far_static = prepare_wide(
        mask_u, mask_v, wave, wind_base, wind_seeds, wind_scale, total_x, total_y
    )
    surface, flow_u, flow_v = (height, transport_u, transport_v)
    thick, speed_u, speed_v = (thickness, velocity_u, velocity_v)
    depth_u = None
    depth_v = None
    for outer in range(STEPS):
        east_h, west_h, south_h, north_h, west_u, south_v = layer_neighbours(
            thick, speed_u, speed_v, top
        )
        thick_u = (thick + east_h) * 0.5
        thick_v = (thick + north_h) * 0.5
        if depth_u is None:
            depth_u = jnp.sum(thick_u, axis=0)
            depth_v = jnp.sum(thick_v, axis=0)
        surface, flow_u, flow_v, mean_u, mean_v = wide_substeps(
            surface, flow_u, flow_v, own_static, far_static, top
        )
        flux_u = speed_u * thick_u
        flux_v = speed_v * thick_v
        west_flux = west_u * (west_h + thick) * 0.5
        south_flux = south_v * (south_h + thick) * 0.5
        pressure = jnp.cumsum(thick, axis=0)
        east_press = jnp.cumsum(east_h, axis=0)
        north_press = jnp.cumsum(north_h, axis=0)
        trial_u = speed_u - PRESS_COEF * (east_press - pressure)
        trial_v = speed_v - PRESS_COEF * (north_press - pressure)
        speed_u = mask_u * (trial_u + (mean_u - jnp.sum(thick_u * trial_u, axis=0)) / depth_u)
        speed_v = mask_v * (trial_v + (mean_v - jnp.sum(thick_v * trial_v, axis=0)) / depth_v)
        thick = thick - FLUX_STEP * (flux_u - west_flux + flux_v - south_flux)
    return (surface, flow_u, flow_v, thick, speed_u, speed_v)


def solution(mesh):
    placed = (
        P(("members", "zonal"), "merid"),
        P(("members", "zonal"), "merid"),
        P(("members", "zonal"), "merid"),
        P(None, ("members", "zonal"), "merid"),
        P(None, ("members", "zonal"), "merid"),
        P(None, ("members", "zonal"), "merid"),
        P(None, "zonal", "merid"),
        P("members", None),
        P("members"),
        P(None, "zonal", "merid"),
    )
    return jax.shard_map(
        body,
        mesh=mesh,
        in_specs=placed,
        out_specs=(
            P(("members", "zonal"), "merid"),
            P(("members", "zonal"), "merid"),
            P(("members", "zonal"), "merid"),
            P(None, ("members", "zonal"), "merid"),
            P(None, ("members", "zonal"), "merid"),
            P(None, ("members", "zonal"), "merid"),
        ),
        check_vma=False,
    )
```

profile of v0, /device:TPU:37, one launch (start us, length us, event | category | flops | bytes accessed | tf_op | source)
XLA Modules:
  0.0 313.8 jit_solution(9494711897709370061)
XLA Ops:
  1.6 2.8 collective-permute-start.13
  5.5 2.0 collective-permute-start.14
  7.4 19.2 %collective-permute-start.12 = (f32[14,1,512]{2,1,0:T(1,128)S(1)}, f32[14,1,512]{2,1,0:T(1,128)S(1)}, u32[]{:S(2)}, u32[]{:S(2)}) collective-permute-start(f32[14,1,512]{2,1,0:T(1,128)S(1)} %get-tuple-element.86), channel_id=1, source_target_pairs={{2,0},{4,2},{6,4},{8,6},{10,8},{12,10},{14,12},{16,14},{18,16},{20... | collective-permute-start | bytes 86024 | tf_op jit(solution)/shard_map/ppermute | solution.py:56
  27.7 1.4 collective-permute-start.16
  32.7 40.1 %all-gather = f32[14,512,1]{0,2,1:T(1,128)S(1)} all-gather(f32[14,16,1]{0,2,1:T(1,128)S(1)} %copy.307), channel_id=2, replica_groups=mesh['members'=4,'zonal'=32,'merid'=2] {'zonal'}, dimensions={1}, use_global_device_ids=true | all-gather | bytes 29568 | tf_op jit(solution)/shard_map/all_gather | solution.py:97
  76.8 3.6 %multiply_reduce_fusion.5 = (f32[30,526]{1,0:T(8,128)}, f32[30,526]{1,0:T(8,128)}) fusion(f32[4,526]{1,0:T(4,128)S(1)} %fusion.71, f32[4,30]{0,1:T(8,128)S(1)} %copy.275, f32[4]{0:T(128)S(1)} %copy-done.41), kind=kLoop, calls=%fused_computation.74 | loop fusion | flops 347160 | bytes 135152 | tf_op jit(solution)/shard_map/reduce_sum | solution.py:90
  80.4 14.4 %collective-permute-start.15 = (f32[14,16,1]{2,1,0:T(8,128)S(1)}, f32[14,16,1]{2,1,0:T(8,128)S(1)}, u32[]{:S(2)}, u32[]{:S(2)}) collective-permute-start(f32[14,16,1]{2,1,0:T(8,128)S(1)} %get-tuple-element.84), channel_id=1, source_target_pairs={{1,0},{0,1},{3,2},{2,3},{5,4},{4,5},{7,6},{6,7},{9,8},{8,9},{11,10... | collective-permute-start | bytes 2696 | tf_op jit(solution)/shard_map/ppermute | solution.py:56
  95.7 2.2 collective-permute-start.1
  100.1 2.2 fusion.117
  102.4 2.6 collective-permute-start.18
  109.6 39.0 %all-gather.1 = f32[14,512,1]{0,2,1:T(1,128)S(1)} all-gather(f32[14,16,1]{0,2,1:T(1,128)S(1)} %copy.293), channel_id=3, replica_groups=mesh['members'=4,'zonal'=32,'merid'=2] {'zonal'}, dimensions={1}, use_global_device_ids=true | all-gather | bytes 29568 | tf_op jit(solution)/shard_map/all_gather | solution.py:97
  148.8 14.0 %collective-permute-start.2 = (f32[3,30,7]{2,1,0:T(8,128)S(1)}, f32[3,30,7]{2,1,0:T(8,128)S(1)}, u32[]{:S(2)}, u32[]{:S(2)}) collective-permute-start(f32[3,30,7]{2,1,0:T(8,128)S(1)} %get-tuple-element.91), channel_id=1, source_target_pairs={{0,1},{1,0},{2,3},{3,2},{4,5},{5,4},{6,7},{7,6},{8,9},{9,8},{10,11... | collective-permute-start | bytes 7568 | tf_op jit(solution)/shard_map/ppermute | solution.py:41
  163.6 1.6 collective-permute-start.4
  167.5 12.5 %all-to-all-start = ((f32[32,1,630]{2,1,0:T(1,128)}), f32[32,1,630]{2,1,0:T(1,128)S(1)}, u32[]{:S(2)}, u32[]{:S(2)}) async-start(f32[32,1,630]{2,1,0:T(1,128)} %reshape.334), calls=%async_computation | async-start | bytes 163840 | tf_op jit(solution)/shard_map/all_to_all | solution.py:20
  180.3 1.3 collective-permute-start.6
  185.8 18.2 %all-to-all-done = f32[32,1,630]{2,1,0:T(1,128)S(1)} async-done(((f32[32,1,630]{2,1,0:T(1,128)}), f32[32,1,630]{2,1,0:T(1,128)S(1)}, u32[]{:S(2)}, u32[]{:S(2)}) %all-to-all-start) | async-done | bytes 80672 | tf_op jit(solution)/shard_map/all_to_all | solution.py:20
  204.0 5.4 %all-to-all-start.1 = ((f32[32,1,1050]{2,1,0:T(1,128)}), f32[32,1,1050]{2,1,0:T(1,128)S(1)}, u32[]{:S(2)}, u32[]{:S(2)}) async-start(f32[32,1,1050]{2,1,0:T(1,128)} %reshape.336), calls=%async_computation.1 | async-start | bytes 294912 | tf_op jit(solution)/shard_map/all_to_all | solution.py:20
  216.3 21.3 %all-to-all-done.1 = f32[32,1,1050]{2,1,0:T(1,128)S(1)} async-done(((f32[32,1,1050]{2,1,0:T(1,128)}), f32[32,1,1050]{2,1,0:T(1,128)S(1)}, u32[]{:S(2)}, u32[]{:S(2)}) %all-to-all-start.1) | async-done | bytes 134432 | tf_op jit(solution)/shard_map/all_to_all | solution.py:20
  252.6 2.4 collective-permute-start.9
  257.5 2.2 multiply_reduce_fusion
  259.8 5.5 %collective-permute-start.10 = (f32[3,30,7]{2,1,0:T(8,128)S(1)}, f32[3,30,7]{2,1,0:T(8,128)S(1)}, u32[]{:S(2)}, u32[]{:S(2)}) collective-permute-start(f32[3,30,7]{2,1,0:T(8,128)S(1)} %get-tuple-element.89), channel_id=1, source_target_pairs={{0,1},{1,0},{2,3},{3,2},{4,5},{5,4},{6,7},{7,6},{8,9},{9,8},{10,11... | collective-permute-start | bytes 7568 | tf_op jit(solution)/shard_map/ppermute | solution.py:41
  265.5 2.6 fusion.14
  269.3 5.5 %all-to-all-start.2 = ((f32[32,1,630]{2,1,0:T(1,128)}), f32[32,1,630]{2,1,0:T(1,128)S(1)}, u32[]{:S(2)}, u32[]{:S(2)}) async-start(f32[32,1,630]{2,1,0:T(1,128)} %reshape.338), calls=%async_computation.2 | async-start | bytes 163840 | tf_op jit(solution)/shard_map/all_to_all | solution.py:20
  275.4 23.4 %all-to-all-done.2 = f32[32,1,630]{2,1,0:T(1,128)S(1)} async-done(((f32[32,1,630]{2,1,0:T(1,128)}), f32[32,1,630]{2,1,0:T(1,128)S(1)}, u32[]{:S(2)}, u32[]{:S(2)}) %all-to-all-start.2) | async-done | bytes 80672 | tf_op jit(solution)/shard_map/all_to_all | solution.py:20
  (350 shorter events, 66.7 us)
Async XLA Ops:
  1.6 96.3 %collective-permute-start.13 = (f32[14,1,512]{2,1,0:T(1,128)S(1)}, f32[14,1,512]{2,1,0:T(1,128)S(1)}, u32[]{:S(2)}, u32[]{:S(2)}) collective-permute-start(f32[14,1,512]{2,1,0:T(1,128)S(1)} %slice.768), channel_id=1, source_target_pairs={{62,0},{0,2},{2,4},{4,6},{6,8},{8,10},{10,12},{12,14},{14,16},{16,... | collective-permute-start | bytes 86024 | tf_op jit(solution)/shard_map/ppermute | solution.py:70
  5.5 92.5 %collective-permute-start.14 = (f32[14,1,512]{2,1,0:T(1,128)S(1)}, f32[14,1,512]{2,1,0:T(1,128)S(1)}, u32[]{:S(2)}, u32[]{:S(2)}) collective-permute-start(f32[14,1,512]{2,1,0:T(1,128)S(1)} %get-tuple-element.85), channel_id=1, source_target_pairs={{0,2},{2,4},{4,6},{6,8},{8,10},{10,12},{12,14},{14,16},{16,18},{18... | collective-permute-start | bytes 86024 | tf_op jit(solution)/shard_map/ppermute | solution.py:55
  7.4 90.5 %collective-permute-start.12 = (f32[14,1,512]{2,1,0:T(1,128)S(1)}, f32[14,1,512]{2,1,0:T(1,128)S(1)}, u32[]{:S(2)}, u32[]{:S(2)}) collective-permute-start(f32[14,1,512]{2,1,0:T(1,128)S(1)} %get-tuple-element.86), channel_id=1, source_target_pairs={{2,0},{4,2},{6,4},{8,6},{10,8},{12,10},{14,12},{16,14},{18,16},{20... | collective-permute-start | bytes 86024 | tf_op jit(solution)/shard_map/ppermute | solution.py:56
  27.7 67.5 %collective-permute-start.16 = (f32[14,16,1]{2,1,0:T(8,128)S(1)}, f32[14,16,1]{2,1,0:T(8,128)S(1)}, u32[]{:S(2)}, u32[]{:S(2)}) collective-permute-start(f32[14,16,1]{2,1,0:T(8,128)S(1)} %slice.775), channel_id=1, source_target_pairs={{0,1},{2,3},{4,5},{6,7},{8,9},{10,11},{12,13},{14,15},{16,17},{18,... | collective-permute-start | bytes 2696 | tf_op jit(solution)/shard_map/ppermute | solution.py:76
  30.4 50.0 %collective-permute-start.17 = (f32[14,16,1]{0,2,1:T(1,128)S(1)}, f32[14,16,1]{0,2,1:T(1,128)S(1)}, u32[]{:S(2)}, u32[]{:S(2)}) collective-permute-start(f32[14,16,1]{0,2,1:T(1,128)S(1)} %copy.307), channel_id=1, source_target_pairs={{0,1},{1,0},{2,3},{3,2},{4,5},{5,4},{6,7},{7,6},{8,9},{9,8},{10,11... | collective-permute-start | bytes 2696 | tf_op jit(solution)/shard_map/ppermute | solution.py:55
  80.4 15.3 %collective-permute-start.15 = (f32[14,16,1]{2,1,0:T(8,128)S(1)}, f32[14,16,1]{2,1,0:T(8,128)S(1)}, u32[]{:S(2)}, u32[]{:S(2)}) collective-permute-start(f32[14,16,1]{2,1,0:T(8,128)S(1)} %get-tuple-element.84), channel_id=1, source_target_pairs={{1,0},{0,1},{3,2},{2,3},{5,4},{4,5},{7,6},{6,7},{9,8},{8,9},{11,10... | collective-permute-start | bytes 2696 | tf_op jit(solution)/shard_map/ppermute | solution.py:56
  95.1 53.5 %collective-permute-start = (f32[3,7,512]{2,1,0:T(8,128)}, f32[3,7,512]{2,1,0:T(8,128)S(1)}, u32[]{:S(2)}, u32[]{:S(2)}) collective-permute-start(f32[3,7,512]{2,1,0:T(8,128)} %get-tuple-element.97), channel_id=1, source_target_pairs={{0,2},{2,4},{4,6},{6,8},{8,10},{10,12},{12,14},{14,16},{16,18},{18... | collective-permute-start | bytes 129032 | tf_op jit(solution)/shard_map/ppermute | solution.py:41
  95.7 52.9 %collective-permute-start.1 = (f32[3,7,512]{2,1,0:T(8,128)S(1)}, f32[3,7,512]{2,1,0:T(8,128)S(1)}, u32[]{:S(2)}, u32[]{:S(2)}) collective-permute-start(f32[3,7,512]{2,1,0:T(8,128)S(1)} %get-tuple-element.98), channel_id=1, source_target_pairs={{2,0},{4,2},{6,4},{8,6},{10,8},{12,10},{14,12},{16,14},{18,16},{20... | collective-permute-start | bytes 129032 | tf_op jit(solution)/shard_map/ppermute | solution.py:42
  102.2 155.1 %collective-permute-start.20 = (f32[14,1,512]{2,1,0:T(1,128)}, f32[14,1,512]{2,1,0:T(1,128)}, u32[]{:S(2)}, u32[]{:S(2)}) collective-permute-start(f32[14,1,512]{2,1,0:T(1,128)} %get-tuple-element.81), channel_id=1, source_target_pairs={{0,2},{2,4},{4,6},{6,8},{8,10},{10,12},{12,14},{14,16},{16,18},{18... | collective-permute-start | bytes 86024 | tf_op jit(solution)/shard_map/ppermute | solution.py:55
  102.4 150.2 %collective-permute-start.18 = (f32[14,1,512]{2,1,0:T(1,128)}, f32[14,1,512]{2,1,0:T(1,128)}, u32[]{:S(2)}, u32[]{:S(2)}) collective-permute-start(f32[14,1,512]{2,1,0:T(1,128)} %get-tuple-element.82), channel_id=1, source_target_pairs={{2,0},{4,2},{6,4},{8,6},{10,8},{12,10},{14,12},{16,14},{18,16},{20... | collective-permute-start | bytes 86024 | tf_op jit(solution)/shard_map/ppermute | solution.py:56
  105.0 160.5 %collective-permute-start.23 = (f32[14,16,1]{2,1,0:T(8,128)}, f32[14,16,1]{2,1,0:T(8,128)}, u32[]{:S(2)}, u32[]{:S(2)}) collective-permute-start(f32[14,16,1]{2,1,0:T(8,128)} %get-tuple-element.79), channel_id=1, source_target_pairs={{0,1},{1,0},{2,3},{3,2},{4,5},{5,4},{6,7},{7,6},{8,9},{9,8},{10,11... | collective-permute-start | bytes 2696 | tf_op jit(solution)/shard_map/ppermute | solution.py:55
  148.8 14.9 %collective-permute-start.2 = (f32[3,30,7]{2,1,0:T(8,128)S(1)}, f32[3,30,7]{2,1,0:T(8,128)S(1)}, u32[]{:S(2)}, u32[]{:S(2)}) collective-permute-start(f32[3,30,7]{2,1,0:T(8,128)S(1)} %get-tuple-element.91), channel_id=1, source_target_pairs={{0,1},{1,0},{2,3},{3,2},{4,5},{5,4},{6,7},{7,6},{8,9},{9,8},{10,11... | collective-permute-start | bytes 7568 | tf_op jit(solution)/shard_map/ppermute | solution.py:41
  163.6 16.5 %collective-permute-start.4 = (f32[5,7,512]{2,1,0:T(8,128)S(1)}, f32[5,7,512]{2,1,0:T(8,128)S(1)}, u32[]{:S(2)}, u32[]{:S(2)}) collective-permute-start(f32[5,7,512]{2,1,0:T(8,128)S(1)} %get-tuple-element.93), channel_id=1, source_target_pairs={{0,2},{2,4},{4,6},{6,8},{8,10},{10,12},{12,14},{14,16},{16,18},{18... | collective-permute-start | bytes 215048 | tf_op jit(solution)/shard_map/ppermute | solution.py:41
  165.2 14.9 %collective-permute-start.5 = (f32[5,7,512]{2,1,0:T(8,128)S(1)}, f32[5,7,512]{2,1,0:T(8,128)S(1)}, u32[]{:S(2)}, u32[]{:S(2)}) collective-permute-start(f32[5,7,512]{2,1,0:T(8,128)S(1)} %get-tuple-element.94), channel_id=1, source_target_pairs={{2,0},{4,2},{6,4},{8,6},{10,8},{12,10},{14,12},{16,14},{18,16},{20... | collective-permute-start | bytes 215048 | tf_op jit(solution)/shard_map/ppermute | solution.py:42
  167.5 36.5 %all-to-all-start = ((f32[32,1,630]{2,1,0:T(1,128)}), f32[32,1,630]{2,1,0:T(1,128)S(1)}, u32[]{:S(2)}, u32[]{:S(2)}) async-start(f32[32,1,630]{2,1,0:T(1,128)} %reshape.334), calls=%async_computation | async-start | bytes 163840 | tf_op jit(solution)/shard_map/all_to_all | solution.py:20
  180.3 3.6 %collective-permute-start.6 = (f32[5,30,7]{2,1,0:T(8,128)S(1)}, f32[5,30,7]{2,1,0:T(8,128)S(1)}, u32[]{:S(2)}, u32[]{:S(2)}) collective-permute-start(f32[5,30,7]{2,1,0:T(8,128)S(1)} %get-tuple-element.87), channel_id=1, source_target_pairs={{0,1},{1,0},{2,3},{3,2},{4,5},{5,4},{6,7},{7,6},{8,9},{9,8},{10,11... | collective-permute-start | bytes 12608 | tf_op jit(solution)/shard_map/ppermute | solution.py:41
  183.9 72.1 %collective-permute-start.21 = (f32[14,16,1]{2,1,0:T(8,128)}, f32[14,16,1]{2,1,0:T(8,128)}, u32[]{:S(2)}, u32[]{:S(2)}) collective-permute-start(f32[14,16,1]{2,1,0:T(8,128)} %get-tuple-element.80), channel_id=1, source_target_pairs={{1,0},{0,1},{3,2},{2,3},{5,4},{4,5},{7,6},{6,7},{9,8},{8,9},{11,10... | collective-permute-start | bytes 2696 | tf_op jit(solution)/shard_map/ppermute | solution.py:56
  204.0 33.6 %all-to-all-start.1 = ((f32[32,1,1050]{2,1,0:T(1,128)}), f32[32,1,1050]{2,1,0:T(1,128)S(1)}, u32[]{:S(2)}, u32[]{:S(2)}) async-start(f32[32,1,1050]{2,1,0:T(1,128)} %reshape.336), calls=%async_computation.1 | async-start | bytes 294912 | tf_op jit(solution)/shard_map/all_to_all | solution.py:20
  251.0 8.7 %collective-permute-start.8 = (f32[3,7,512]{2,1,0:T(8,128)S(1)}, f32[3,7,512]{2,1,0:T(8,128)S(1)}, u32[]{:S(2)}, u32[]{:S(2)}) collective-permute-start(f32[3,7,512]{2,1,0:T(8,128)S(1)} %get-tuple-element.95), channel_id=1, source_target_pairs={{0,2},{2,4},{4,6},{6,8},{8,10},{10,12},{12,14},{14,16},{16,18},{18... | collective-permute-start | bytes 129032 | tf_op jit(solution)/shard_map/ppermute | solution.py:41
  252.6 7.1 %collective-permute-start.9 = (f32[3,7,512]{2,1,0:T(8,128)S(1)}, f32[3,7,512]{2,1,0:T(8,128)S(1)}, u32[]{:S(2)}, u32[]{:S(2)}) collective-permute-start(f32[3,7,512]{2,1,0:T(8,128)S(1)} %get-tuple-element.96), channel_id=1, source_target_pairs={{2,0},{4,2},{6,4},{8,6},{10,8},{12,10},{14,12},{16,14},{18,16},{20... | collective-permute-start | bytes 129032 | tf_op jit(solution)/shard_map/ppermute | solution.py:42
  256.0 9.4 %collective-permute-start.22 = (f32[14,16,1]{2,1,0:T(8,128)S(1)}, f32[14,16,1]{2,1,0:T(8,128)S(1)}, u32[]{:S(2)}, u32[]{:S(2)}) collective-permute-start(f32[14,16,1]{2,1,0:T(8,128)S(1)} %slice.896), channel_id=1, source_target_pairs={{0,1},{2,3},{4,5},{6,7},{8,9},{10,11},{12,13},{14,15},{16,17},{18,... | collective-permute-start | bytes 2696 | tf_op jit(solution)/shard_map/ppermute | solution.py:76
  257.4 8.1 %collective-permute-start.19 = (f32[14,1,512]{2,1,0:T(1,128)S(1)}, f32[14,1,512]{2,1,0:T(1,128)S(1)}, u32[]{:S(2)}, u32[]{:S(2)}) collective-permute-start(f32[14,1,512]{2,1,0:T(1,128)S(1)} %slice.885), channel_id=1, source_target_pairs={{62,0},{0,2},{2,4},{4,6},{6,8},{8,10},{10,12},{12,14},{14,16},{16,... | collective-permute-start | bytes 86024 | tf_op jit(solution)/shard_map/ppermute | solution.py:70
  259.8 8.3 %collective-permute-start.10 = (f32[3,30,7]{2,1,0:T(8,128)S(1)}, f32[3,30,7]{2,1,0:T(8,128)S(1)}, u32[]{:S(2)}, u32[]{:S(2)}) collective-permute-start(f32[3,30,7]{2,1,0:T(8,128)S(1)} %get-tuple-element.89), channel_id=1, source_target_pairs={{0,1},{1,0},{2,3},{3,2},{4,5},{5,4},{6,7},{7,6},{8,9},{9,8},{10,11... | collective-permute-start | bytes 7568 | tf_op jit(solution)/shard_map/ppermute | solution.py:41
  269.3 29.4 %all-to-all-start.2 = ((f32[32,1,630]{2,1,0:T(1,128)}), f32[32,1,630]{2,1,0:T(1,128)S(1)}, u32[]{:S(2)}, u32[]{:S(2)}) async-start(f32[32,1,630]{2,1,0:T(1,128)} %reshape.338), calls=%async_computation.2 | async-start | bytes 163840 | tf_op jit(solution)/shard_map/all_to_all | solution.py:20
  (45 other events, 172.3 us)
where the time goes:
time: 318 us; the launch traced here: 314 us
  starting transfers between devices  99.5 us (31%)
  blocking collectives  79.2 us (25%)
  waiting for transfers between devices  63.1 us (20%)
  other arithmetic  37.3 us (12%)
  local copies, waits for them, and re-layouts  33.2 us (10%)
    all_gather x2, blocking collectives, mirror_layers(): whole = lax.all_gather(top_rows, 'zonal', axis=1, tiled=True)  79.2 us
    all_to_all x3, waiting for transfers between devices, sent_to_all(): return lax.all_to_all(copies, axis, split_axis=0, concat_axis=0, tiled=True)  62.9 us
    ppermute x4, starting transfers between devices, padded_2(): lax.ppermute(leading, axis, [(b, a) for a, b in up])  36.6 us
    all_to_all x3, starting transfers between devices, sent_to_all(): return lax.all_to_all(copies, axis, split_axis=0, concat_axis=0, tiled=True)  23.4 us
    ppermute x6, starting transfers between devices, extended(): before = lax.ppermute(last, axis, up)  23.2 us
    unnamed x97, local copies, waits for them, and re-layouts  11.3 us
    mul x21, other arithmetic, update_flows(): mask_u * (state[1] - wave * (from_high(surface, 0) - surface) + stress_x)  9.63 us
  transfers between devices with their start and end apart: 27, of which 4 were waited for; matrix products, arithmetic and copies ran while one was open for 15% of the time, Pallas kernels for 0%

commit v1 on v0

v1 whole, which is shorter than its diff:
```python
import functools
import math

import jax
import jax.numpy as jnp
from jax import lax
from jax.experimental import pallas as pl
from jax.experimental.pallas import tpu as pltpu
from jax.sharding import PartitionSpec as P

NSUB = 6
STEPS = 2
WAVE_LIMIT = 0.225
STRESS_SCALE = 0.1
FLUX_STEP = 0.05
PRESS_COEF = 0.05

MESH = pl.DeviceIdType.MESH
F32 = jnp.float32
OWN, EAST, WEST = 0, 1, 2
LANES = 128
STRIP = 16


def lane_iota(shape):
    return lax.broadcasted_iota(jnp.int32, shape, len(shape) - 1)


def modulo(value, size):
    return value & (size - 1) if size & (size - 1) == 0 else lax.rem(value, size)


def exchange(
    sizes,
    eta_ref, bu_ref, bv_ref, h_ref, u_ref, v_ref, faces_ref, base_ref, seeds_ref, scale_ref,
    own_ref, east_ref, west_ref, least_ref, lwest_ref, north_ref, south_ref,
    goeast, gowest, top, bottom, send, recv,
):
    devices = sizes
    z = lax.axis_index("zonal")
    c = lax.axis_index("merid")
    e = lax.rem(z + 1, devices)
    w = lax.rem(z + devices - 1, devices)
    other = 1 - c
    far = [lax.rem(2 * devices - 1 - z + d, devices) for d in (0, -1, 1)]

    barrier = pltpu.get_barrier_semaphore()

    def greet(zonal, merid):
        pl.semaphore_signal(
            barrier, inc=1, device_id={"zonal": zonal, "merid": merid}, device_id_type=MESH
        )

    greet(e, c)
    greet(w, c)
    for target in (z, e, w):
        greet(target, other)
    for target in far:
        @pl.when(jnp.logical_and(c == 1, target != z))
        def _(target=target):
            greet(target, c)

    layers, cells, rows = h_ref.shape
    total_x = cells * devices
    total_y = rows * 2
    h_sum = h_ref[0]
    for l in range(1, layers):
        h_sum = h_sum + h_ref[l]
    wave = (WAVE_LIMIT / layers) * h_sum
    mask_u = faces_ref[0].astype(F32)
    mask_v = faces_ref[1].astype(F32)
    cols = lax.broadcasted_iota(jnp.int32, (cells, LANES), 0) + z * cells
    rws = lax.broadcasted_iota(jnp.int32, (8, rows), 1) + c * rows
    sum_cos = jnp.zeros((cells, rows), F32)
    sum_sin = jnp.zeros((cells, rows), F32)
    for m in range(seeds_ref.shape[0]):
        ax = (2.0 * math.pi / total_x) * modulo(seeds_ref[m, 0] * cols, total_x).astype(F32)
        ay = (2.0 * math.pi / total_y) * modulo(seeds_ref[m, 1] * rws, total_y).astype(F32)
        amp = scale_ref[m]
        cx = jnp.concatenate([amp * jnp.cos(ax)] * (rows // LANES), 1)
        sx = jnp.concatenate([amp * jnp.sin(ax)] * (rows // LANES), 1)
        cy = jnp.concatenate([jnp.cos(ay)] * (cells // 8), 0)
        sy = jnp.concatenate([jnp.sin(ay)] * (cells // 8), 0)
        sum_cos = sum_cos + (cx * cy - sx * sy)
        sum_sin = sum_sin + (sx * cy + cx * sy)
    own_ref[0] = mask_u * wave
    own_ref[1] = mask_v * wave
    own_ref[2] = mask_u * (STRESS_SCALE * (base_ref[0] + sum_cos))
    own_ref[3] = mask_v * (STRESS_SCALE * (base_ref[1] + sum_sin))
    own_ref[4] = eta_ref[...]
    own_ref[5] = bu_ref[...]
    own_ref[6] = bv_ref[...]
    pad = jnp.zeros((16 - layers, rows), F32)
    last = cells - 1
    for k, (ref, col) in enumerate(((h_ref, last), (h_ref, last - 1), (u_ref, last), (u_ref, last - 1), (v_ref, last))):
        goeast[k] = jnp.concatenate([ref[:, col, :], pad], 0)
    for k, (ref, col) in enumerate(((h_ref, 0), (h_ref, 1), (u_ref, 0), (v_ref, 0))):
        gowest[k] = jnp.concatenate([ref[:, col, :], pad], 0)
    lane = lane_iota((cells, LANES))
    hi = rows - LANES
    base_t = jnp.zeros((cells, LANES), F32)
    base_b = jnp.zeros((cells, LANES), F32)
    for f in range(7):
        here = lane // STRIP == f
        base_t = jnp.where(here, pltpu.roll(own_ref[f, :, hi:], (f * STRIP + STRIP) % LANES, 1), base_t)
        low = own_ref[f, :, :LANES]
        base_b = jnp.where(here, pltpu.roll(low, f * STRIP, 1) if f else low, base_b)
    lay_t = jnp.zeros((cells, LANES), F32)
    lay_b = jnp.zeros((cells, LANES), F32)
    for start, width, ref in ((0, 2, h_ref), (2 * layers, 2, v_ref), (4 * layers, 1, u_ref)):
        for l in range(layers):
            spot = start + width * l
            here = jnp.logical_and(lane >= spot, lane < spot + width)
            lay_t = jnp.where(here, pltpu.roll(ref[l, :, hi:], (spot + width) % LANES, 1), lay_t)
            low = ref[l, :, :LANES]
            lay_b = jnp.where(here, pltpu.roll(low, spot, 1) if spot else low, lay_b)
    bottom[:, :LANES] = base_b
    bottom[:, LANES:] = lay_b
    r2 = lax.broadcasted_iota(jnp.int32, (LANES, LANES), 0)
    c2 = lax.broadcasted_iota(jnp.int32, (LANES, LANES), 1)
    perm_b = jnp.where(r2 == (c2 ^ (STRIP - 1)), 1.0, 0.0).astype(F32)
    perm_l = jnp.where(r2 == jnp.where(c2 < 4 * layers, c2 ^ 1, c2), 1.0, 0.0).astype(F32)
    r1 = lax.broadcasted_iota(jnp.int32, (cells, cells), 0)
    c1 = lax.broadcasted_iota(jnp.int32, (cells, cells), 1)
    mirror = jnp.where(r1 + c1 == cells - 1, 1.0, 0.0).astype(F32)
    dot = functools.partial(
        jnp.dot, preferred_element_type=F32, precision=lax.Precision.HIGHEST
    )
    north_edge = c == 1
    top[:, :LANES] = jnp.where(north_edge, dot(mirror, dot(base_t, perm_b)), base_t)
    top[:, LANES:] = jnp.where(north_edge, dot(mirror, dot(lay_t, perm_l)), lay_t)

    @pl.when(c == 0)
    def _():
        south_ref[...] = jnp.zeros_like(south_ref)

    for target, slot in zip(far, (OWN, EAST, WEST)):
        @pl.when(jnp.logical_and(c == 1, target == z))
        def _(slot=slot):
            north_ref[slot] = top[...]

    alone = sum(jnp.where(target == z, 1, 0) for target in far)
    pl.semaphore_wait(barrier, 5 + c * (3 - alone))

    def copy(src, dst, k, zonal, merid):
        return pltpu.make_async_remote_copy(
            src_ref=src, dst_ref=dst, send_sem=send.at[k], recv_sem=recv.at[k],
            device_id={"zonal": zonal, "merid": merid}, device_id_type=MESH,
        )

    far_copies = [
        copy(top, north_ref.at[slot], 4 + slot, target, c)
        for target, slot in zip(far, (OWN, EAST, WEST))
    ]
    up_copies = [
        copy(top, south_ref.at[slot], 7 + slot, target, other)
        for target, slot in zip((z, w, e), (OWN, EAST, WEST))
    ]
    down_copies = [
        copy(bottom, north_ref.at[slot], 10 + slot, target, other)
        for target, slot in zip((z, w, e), (OWN, EAST, WEST))
    ]
    side_copies = [
        copy(goeast, lwest_ref, 0, e, c),
        copy(gowest, least_ref, 1, w, c),
        copy(own_ref, west_ref, 2, e, c),
        copy(own_ref, east_ref, 3, w, c),
    ]
    for target, cp in zip(far, far_copies):
        @pl.when(jnp.logical_and(c == 1, target != z))
        def _(cp=cp):
            cp.start()

    @pl.when(c == 0)
    def _():
        for cp in up_copies:
            cp.start()

    @pl.when(c == 1)
    def _():
        for cp in down_copies:
            cp.start()

    for cp in side_copies:
        cp.start()
    for cp in side_copies:
        cp.wait()

    @pl.when(c == 0)
    def _():
        for cp in up_copies:
            cp.wait_send()
        for cp in down_copies:
            cp.wait_recv()

    @pl.when(c == 1)
    def _():
        for cp in down_copies:
            cp.wait_send()
        for cp in up_copies:
            cp.wait_recv()

    for target, cp in zip(far, far_copies):
        @pl.when(jnp.logical_and(c == 1, target != z))
        def _(cp=cp):
            cp.wait()


def advance(
    h_ref, u_ref, v_ref, own_ref, east_ref, west_ref, least_ref, lwest_ref, north_ref, south_ref,
    eta_out, bu_out, bv_out, h_out, u_out, v_out,
    base, lay, trial,
):
    layers, cells, rows = h_ref.shape
    wide = rows + LANES
    lane = lane_iota((cells, LANES))
    first = lane < LANES // 2
    fold1 = jnp.logical_and(lane_iota((8, LANES)) < LANES // 2, lax.axis_index("merid") == 1)

    def rolled(x, shift, axis):
        shift = shift % x.shape[axis]
        return pltpu.roll(x, shift, axis) if shift else x

    def fold_of(x):
        return jnp.concatenate([fold1] * (x.shape[0] // 8), 0)

    def merge(main, alt):
        halo = jnp.where(fold_of(alt), alt, main[:, rows:])
        return jnp.concatenate([main[:, :rows], halo], 1)

    def at_west(x):
        return merge(rolled(x, 1, 0), rolled(x[:, rows:], -1, 0))

    def at_east(x):
        return merge(rolled(x, -1, 0), rolled(x[:, rows:], 1, 0))

    def at_south(x):
        return merge(rolled(x, 1, 1), rolled(x[:, rows:], -1, 1))

    def at_north(x):
        return merge(rolled(x, -1, 1), rolled(x[:, rows - LANES:], 1, 1)[:, LANES:])

    for f in range(7):
        for slot, ref in ((OWN, own_ref), (EAST, east_ref), (WEST, west_ref)):
            place = slice(slot * cells, (slot + 1) * cells)
            base[f, place, :rows] = ref[f]
            base[f, place, rows:] = jnp.where(
                first,
                rolled(north_ref[slot, :, :LANES], -STRIP * f, 1),
                rolled(south_ref[slot, :, :LANES], LANES - STRIP - STRIP * f, 1),
            )
    near = lax.broadcasted_iota(jnp.int32, (8, LANES), 0) < 4

    def around(x):
        return jnp.concatenate([x[OWN], jnp.where(near, x[EAST][:8], x[WEST][cells - 8:])], 0)

    north = around([north_ref[s, :, LANES:] for s in range(3)])
    south = around([south_ref[s, :, LANES:] for s in range(3)])
    first24 = lane_iota(north.shape) < LANES // 2
    ext = cells + 8
    H, U, V = 0, 1, 2
    for kind, ref, start, width, east_cols, west_cols in (
        (H, h_ref, 0, 2, (0, 1), (0, 1)),
        (U, u_ref, 4 * layers, 1, (2,), (2, 3)),
        (V, v_ref, 2 * layers, 2, (3,), (4,)),
    ):
        for l in range(layers):
            spot = start + width * l
            lay[kind, l, :cells, :rows] = ref[l]
            lay[kind, l, cells:, :rows] = jnp.zeros((8, rows), F32)
            lay[kind, l, :, rows:] = jnp.where(
                first24, rolled(north, -spot, 1), rolled(south, LANES - width - spot, 1)
            )
            for k, src in enumerate(east_cols):
                lay[kind, l, cells + k: cells + k + 1, :rows] = least_ref[src, l: l + 1, :]
            for k, src in enumerate(west_cols):
                lay[kind, l, ext - 1 - k: ext - k, :rows] = lwest_ref[src, l: l + 1, :]

    def trimmed(x):
        wide_near = lax.broadcasted_iota(jnp.int32, (8, wide), 0) < 4
        return jnp.concatenate([x[:cells], jnp.where(wide_near, x[cells: cells + 8], x[3 * cells - 8:])], 0)

    mask_u = trimmed(base[0]) != 0.0
    mask_v = trimmed(base[1]) != 0.0
    depth_u = None
    depth_v = None
    for outer in range(STEPS):
        def substep(_, sums):
            sum_u, sum_v = sums
            bu = base[5]
            bv = base[6]
            eta = base[4] - (bu - at_west(bu) + bv - at_south(bv))
            base[4] = eta
            au = base[0]
            bu = jnp.where(au != 0.0, bu - au * (at_east(eta) - eta) + base[2], 0.0)
            base[5] = bu
            av = base[1]
            bv = jnp.where(av != 0.0, bv - av * (at_north(eta) - eta) + base[3], 0.0)
            base[6] = bv
            return sum_u + trimmed(bu), sum_v + trimmed(bv)

        zero = jnp.zeros((ext, wide), F32)
        sum_u, sum_v = lax.fori_loop(0, NSUB, substep, (zero, zero))
        press_u = zero
        press_v = zero
        deep_u = zero
        deep_v = zero
        total_u = zero
        total_v = zero
        for l in range(layers):
            h = lay[H, l]
            u = lay[U, l]
            v = lay[V, l]
            diff_u = at_east(h) - h
            diff_v = at_north(h) - h
            press_u = press_u + diff_u
            press_v = press_v + diff_v
            hu = h + 0.5 * diff_u
            hv = h + 0.5 * diff_v
            flux_u = u * hu
            flux_v = v * hv
            new = h - FLUX_STEP * (flux_u - at_west(flux_u) + flux_v - at_south(flux_v))
            if outer == STEPS - 1:
                h_out[l] = new[:cells, :rows]
            else:
                lay[H, l] = new
            ut = u - PRESS_COEF * press_u
            vt = v - PRESS_COEF * press_v
            trial[0, l] = ut
            trial[1, l] = vt
            total_u = total_u + hu * ut
            total_v = total_v + hv * vt
            if outer == 0:
                deep_u = deep_u + hu
                deep_v = deep_v + hv
        if outer == 0:
            depth_u, depth_v = deep_u, deep_v
        fix_u = (sum_u * (1.0 / NSUB) - total_u) / depth_u
        fix_v = (sum_v * (1.0 / NSUB) - total_v) / depth_v
        for l in range(layers):
            u = jnp.where(mask_u, trial[0, l] + fix_u, 0.0)
            v = jnp.where(mask_v, trial[1, l] + fix_v, 0.0)
            if outer == STEPS - 1:
                u_out[l] = u[:cells, :rows]
                v_out[l] = v[:cells, :rows]
            else:
                lay[U, l] = u
                lay[V, l] = v
    eta_out[...] = base[4, :cells, :rows]
    bu_out[...] = base[5, :cells, :rows]
    bv_out[...] = base[6, :cells, :rows]


def body(
    devices, height, transport_u, transport_v, thickness, velocity_u, velocity_v,
    sea_faces, wind_seeds, wind_scale, wind_base,
):
    layers, cells, rows = thickness.shape
    vmem = pl.BlockSpec(memory_space=pltpu.VMEM)
    smem = pl.BlockSpec(memory_space=pltpu.SMEM)

    def shape(*dims):
        return jax.ShapeDtypeStruct(dims, F32)

    halos = pl.pallas_call(
        functools.partial(exchange, devices),
        out_shape=[
            shape(7, cells, rows), shape(7, cells, rows), shape(7, cells, rows),
            shape(4, 16, rows), shape(5, 16, rows),
            shape(3, cells, 2 * LANES), shape(3, cells, 2 * LANES),
        ],
        in_specs=[vmem] * 8 + [smem] * 2,
        out_specs=[vmem] * 7,
        scratch_shapes=[
            pltpu.VMEM((5, 16, rows), F32),
            pltpu.VMEM((4, 16, rows), F32),
            pltpu.VMEM((cells, 2 * LANES), F32),
            pltpu.VMEM((cells, 2 * LANES), F32),
            pltpu.SemaphoreType.DMA((13,)),
            pltpu.SemaphoreType.DMA((13,)),
        ],
        compiler_params=pltpu.CompilerParams(collective_id=0, has_side_effects=True),
        name="exchange",
    )(
        height, transport_u, transport_v, thickness, velocity_u, velocity_v,
        sea_faces, wind_base, wind_seeds, wind_scale,
    )
    return pl.pallas_call(
        advance,
        out_shape=[shape(cells, rows)] * 3 + [shape(layers, cells, rows)] * 3,
        in_specs=[vmem] * 10,
        out_specs=[vmem] * 6,
        scratch_shapes=[
            pltpu.VMEM((7, 3 * cells, rows + LANES), F32),
            pltpu.VMEM((3, layers, cells + 8, rows + LANES), F32),
            pltpu.VMEM((2, layers, cells + 8, rows + LANES), F32),
        ],
        name="advance",
    )(thickness, velocity_u, velocity_v, *halos)


def solution(mesh):
    flat = P(("members", "zonal"), "merid")
    deep = P(None, ("members", "zonal"), "merid")
    fixed = P(None, "zonal", "merid")
    return jax.shard_map(
        functools.partial(body, mesh.shape["zonal"]),
        mesh=mesh,
        in_specs=(flat, flat, flat, deep, deep, deep, fixed, P("members", None), P("members"), fixed),
        out_specs=(flat, flat, flat, deep, deep, deep),
        check_vma=False,
    )
```

time: 318 us -> 52.2 us (0.16); the launches traced: 314 us -> 52 us
  starting transfers between devices: 99.5 us -> 0 us
  blocking collectives: 79.2 us -> 0 us
  waiting for transfers between devices: 63.1 us -> 0 us
  Pallas kernels: 0 us -> 50 us
  other arithmetic: 37.3 us -> 0 us
  local copies, waits for them, and re-layouts: 33.2 us -> 1.34 us
    all_gather x2 -> x0, blocking collectives: 79.2 us -> none  [mirror_layers(): whole = lax.all_gather(top_rows, 'zonal', axis=1, tiled=True)]
    ppermute x24 -> x0, starting transfers between devices: 76.1 us -> none  [the longest x4 36.6 us: padded_2(): lax.ppermute(leading, axis, [(b, a) for a, b in up])]
    all_to_all x3 -> x0, waiting for transfers between devices: 62.9 us -> none  [sent_to_all(): return lax.all_to_all(copies, axis, split_axis=0, concat_axis=0, tiled=True)]
    pallas_call x0 -> x2, Pallas kernels: none -> 50 us  [the longest x1 41.2 us: body(): pl.pallas_call(functools.partial(exchange, devices), out_shape=[shape(7,...]
    all_to_all x3 -> x0, starting transfers between devices: 23.4 us -> none  [sent_to_all(): return lax.all_to_all(copies, axis, split_axis=0, concat_axis=0, tiled=True)]
    slice x78 -> x0, local copies, waits for them, and re-layouts: 15.3 us -> none  [the longest x44 4.93 us: from_high(): lax.slice_in_dim(field, 1, length, axis=axis)]
    mul x29 -> x0, other arithmetic: 12.9 us -> none  [the longest x21 9.63 us: update_flows(): mask_u * (state[1] - wave * (from_high(surface, 0) - surface) + stress_x)]
    unnamed x97 -> x1, local copies, waits for them, and re-layouts: 11.3 us -> 1.34 us
  transfers between devices with their start and end apart: 27 -> 0, of which waited for: 4 -> 0; matrix products, arithmetic and copies ran while one was open for 15% -> 0% of each run, Pallas kernels for 0% -> 0%
where the time goes in v1:
time: 52.2 us; the launch traced here: 52 us
  Pallas kernels  50 us (96%)
  local copies, waits for them, and re-layouts  1.34 us (3%)
  between operations  0.64 us (1%)
    pallas_call x1, Pallas kernels, body(): pl.pallas_call(functools.partial(exchange, devices), out_shape=[shape(7,...  41.2 us
    pallas_call x1, Pallas kernels, body(): pl.pallas_call(advance, out_shape=[shape(cells, rows)] * 3 + [shape(layer...  8.8 us
    unnamed x1, local copies, waits for them, and re-layouts  1.34 us

profile of v1, /device:TPU:37, one launch (start us, length us, event | category | flops | bytes accessed | tf_op | source)
XLA Modules:
  0.0 52.0 jit_solution(1874206815647190437)
XLA Ops:
  0.6 1.3 %copy.16.seeds_ref = s32[4,2]{1,0:T(4,128)} copy(s32[4,2]{0,1:T(2,128)} %param.17) | data formatting | bytes 64 | tf_op args[7]
  2.0 41.2 %exchange.1 = (f32[7,16,512]{2,1,0:T(8,128)}, f32[7,16,512]{2,1,0:T(8,128)}, f32[7,16,512]{2,1,0:T(8,128)}, f32[4,16,512]{2,1,0:T(8,128)}, f32[5,16,512]{2,1,0:T...) custom-call(f32[16,512]{1,0:T(8,128)} %eta_ref.1, f32[16,512]{1,0:T(8,128)} %bu_ref.1, f32[16,512]{1,0:T(8,128)} %bv_ref.1, ...), custom_call_target="tpu_custom_call" | custom-call | tf_op jit(solution)/shard_map/exchange/pallas_call | solution.py:365
  43.2 8.8 %advance.1 = (f32[16,512]{1,0:T(8,128)}, f32[16,512]{1,0:T(8,128)}, f32[16,512]{1,0:T(8,128)}, f32[14,16,512]{2,1,0:T(8,128)}, f32[14,16,512]{2,1,0:T(8,128)}, /*index=5*/f32[14,16,512]{2,1,0:T(8,128)}) custom-call(f32[14,16,512]{2,1,0:T(8,128)} %h_ref.3, f32[14,16,512]{2,1,0:T(8,128)} %u_ref.3, f32[14,16,512]{2,1,0:T(8,128)} %v_ref.3, ...), custom_call_target="tpu_custom_call" | custom-call | tf_op jit(solution)/shard_map/advance/pallas_call | solution.py:388

commit v2 on v1

v2 whole, which is shorter than its diff:
```python
import functools
import math

import jax
import jax.numpy as jnp
from jax import lax
from jax.experimental import pallas as pl
from jax.experimental.pallas import tpu as pltpu
from jax.sharding import PartitionSpec as P

NSUB = 6
STEPS = 2
WAVE_LIMIT = 0.225
STRESS_SCALE = 0.1
FLUX_STEP = 0.05
PRESS_COEF = 0.05

MESH = pl.DeviceIdType.MESH
F32 = jnp.float32
OWN, EAST, WEST = 0, 1, 2
LANES = 128
STRIP = 16


def lane_iota(shape):
    return lax.broadcasted_iota(jnp.int32, shape, len(shape) - 1)


def modulo(value, size):
    return value & (size - 1) if size & (size - 1) == 0 else lax.rem(value, size)


def rolled(x, shift, axis):
    shift = shift % x.shape[axis]
    return pltpu.roll(x, shift, axis) if shift else x


def neighbours(rows):
    fold1 = jnp.logical_and(lane_iota((8, LANES)) < LANES // 2, lax.axis_index("merid") == 1)

    def merge(main, alt):
        fold = jnp.concatenate([fold1] * (alt.shape[0] // 8), 0)
        halo = jnp.where(fold, alt, main[:, rows:])
        return jnp.concatenate([main[:, :rows], halo], 1)

    def at_west(x):
        return merge(rolled(x, 1, 0), rolled(x[:, rows:], -1, 0))

    def at_east(x):
        return merge(rolled(x, -1, 0), rolled(x[:, rows:], 1, 0))

    def at_south(x):
        return merge(rolled(x, 1, 1), rolled(x[:, rows:], -1, 1))

    def at_north(x):
        return merge(rolled(x, -1, 1), rolled(x[:, rows - LANES:], 1, 1)[:, LANES:])

    return at_east, at_west, at_south, at_north


def exchange(
    devices,
    eta_ref, bu_ref, bv_ref, h_ref, u_ref, v_ref, faces_ref, base_ref, seeds_ref, scale_ref,
    lay, means, faces_out, state_out,
    base, faces, winds, seeds, scale, goeast, gowest, least, lwest, outw, oute, inw, ine,
    top, bottom, north_ref, south_ref,
    load, send, recv, near_ok, far_ok,
):
    z = lax.axis_index("zonal")
    c = lax.axis_index("merid")
    e = lax.rem(z + 1, devices)
    w = lax.rem(z + devices - 1, devices)
    other = 1 - c
    far = [lax.rem(2 * devices - 1 - z + d, devices) for d in (0, -1, 1)]
    layers, cells, rows = h_ref.shape
    wide = rows + LANES
    ext = cells + 8
    H, U, V = 0, 1, 2

    barrier = pltpu.get_barrier_semaphore()

    def greet(zonal, merid):
        pl.semaphore_signal(
            barrier, inc=1, device_id={"zonal": zonal, "merid": merid}, device_id_type=MESH
        )

    greet(e, 1)
    greet(w, 1)

    @pl.when(c == 0)
    def _():
        greet(z, 1)

    @pl.when(c == 1)
    def _():
        for target in far:
            greet(target, 0)

    fetches = [
        pltpu.make_async_copy(src, dst, load.at[k])
        for k, (src, dst) in enumerate((
            (h_ref, lay.at[H, :, pl.ds(0, cells), pl.ds(0, rows)]),
            (seeds_ref, seeds),
            (scale_ref, scale),
            (faces_ref, faces),
            (base_ref, winds),
            (eta_ref, base.at[4, pl.ds(0, cells), pl.ds(0, rows)]),
            (bu_ref, base.at[5, pl.ds(0, cells), pl.ds(0, rows)]),
            (bv_ref, base.at[6, pl.ds(0, cells), pl.ds(0, rows)]),
            (u_ref, lay.at[U, :, pl.ds(0, cells), pl.ds(0, rows)]),
            (v_ref, lay.at[V, :, pl.ds(0, cells), pl.ds(0, rows)]),
        ))
    ]
    for cp in fetches:
        cp.start()
    for cp in fetches[1:5]:
        cp.wait()
    total_x = cells * devices
    total_y = rows * 2
    cols = lax.broadcasted_iota(jnp.int32, (cells, LANES), 0) + z * cells
    rws = lax.broadcasted_iota(jnp.int32, (8, rows), 1) + c * rows
    sum_cos = jnp.zeros((cells, rows), F32)
    sum_sin = jnp.zeros((cells, rows), F32)
    for m in range(seeds.shape[1]):
        ax = (2.0 * math.pi / total_x) * modulo(seeds[0, m] * cols, total_x).astype(F32)
        ay = (2.0 * math.pi / total_y) * modulo(seeds[1, m] * rws, total_y).astype(F32)
        amp = scale[m]
        cx = jnp.concatenate([amp * jnp.cos(ax)] * (rows // LANES), 1)
        sx = jnp.concatenate([amp * jnp.sin(ax)] * (rows // LANES), 1)
        cy = jnp.concatenate([jnp.cos(ay)] * (cells // 8), 0)
        sy = jnp.concatenate([jnp.sin(ay)] * (cells // 8), 0)
        sum_cos = sum_cos + (cx * cy - sx * sy)
        sum_sin = sum_sin + (sx * cy + cx * sy)
    mask_u = faces[0].astype(F32)
    mask_v = faces[1].astype(F32)
    base[2, :cells, :rows] = mask_u * (STRESS_SCALE * (winds[0] + sum_cos))
    base[3, :cells, :rows] = mask_v * (STRESS_SCALE * (winds[1] + sum_sin))
    fetches[0].wait()
    h_sum = lay[H, 0, :cells, :rows]
    for l in range(1, layers):
        h_sum = h_sum + lay[H, l, :cells, :rows]
    wave = (WAVE_LIMIT / layers) * h_sum
    base[0, :cells, :rows] = mask_u * wave
    base[1, :cells, :rows] = mask_v * wave
    for cp in fetches[5:]:
        cp.wait()
    low4 = lax.broadcasted_iota(jnp.int32, (8, rows), 0) < 4
    for k in range(4):
        a = base[2 * k, 0:8, :rows]
        b = base[2 * k, 8:16, :rows]
        if 2 * k + 1 < 7:
            a = jnp.where(low4, pltpu.roll(base[2 * k + 1, 0:8, :rows], 4, 0), a)
            b = jnp.where(low4, b, pltpu.roll(base[2 * k + 1, 8:16, :rows], 4, 0))
        oute[k] = a
        outw[k] = b
    last = cells - 1
    for k, (kind, col) in enumerate(((H, last), (H, last - 1), (U, last), (U, last - 1), (V, last))):
        goeast[k * layers: (k + 1) * layers] = lay[kind, :, col, :rows]
    for k, (kind, col) in enumerate(((H, 0), (H, 1), (U, 0), (V, 0))):
        gowest[k * layers: (k + 1) * layers] = lay[kind, :, col, :rows]

    def copy(src, dst, k, zonal, merid):
        return pltpu.make_async_remote_copy(
            src_ref=src, dst_ref=dst, send_sem=send.at[k], recv_sem=recv.at[k],
            device_id={"zonal": zonal, "merid": merid}, device_id_type=MESH,
        )

    lanes = pl.ds(0, rows)
    side_copies = [
        copy(base.at[:, pl.ds(8, 8), lanes], base.at[:, pl.ds(32, 8), lanes], 0, e, c),
        copy(base.at[:, pl.ds(0, 8), lanes], base.at[:, pl.ds(16, 8), lanes], 1, w, c),
        copy(oute, inw, 2, e, c),
        copy(outw, ine, 3, w, c),
    ]
    column_copies = [
        copy(goeast, lwest, 13, e, c),
        copy(gowest, least, 14, w, c),
    ]

    @pl.when(c == 1)
    def _():
        pl.semaphore_wait(barrier, 5)
        pl.semaphore_signal(
            near_ok, inc=1, device_id={"zonal": z, "merid": other}, device_id_type=MESH
        )

    @pl.when(c == 0)
    def _():
        pl.semaphore_wait(near_ok, 1)

    for cp in side_copies:
        cp.start()
    lane = lane_iota((cells, LANES))
    hi = rows - LANES
    base_t = jnp.zeros((cells, LANES), F32)
    base_b = jnp.zeros((cells, LANES), F32)
    for f in range(7):
        here = lane // STRIP == f
        base_t = jnp.where(here, rolled(base[f, :cells, hi:rows], f * STRIP + STRIP, 1), base_t)
        base_b = jnp.where(here, rolled(base[f, :cells, :LANES], f * STRIP, 1), base_b)
    lay_t = jnp.zeros((cells, LANES), F32)
    lay_b = jnp.zeros((cells, LANES), F32)
    for start, width, kind in ((0, 2, H), (2 * layers, 2, V), (4 * layers, 1, U)):
        for l in range(layers):
            spot = start + width * l
            here = jnp.logical_and(lane >= spot, lane < spot + width)
            lay_t = jnp.where(here, rolled(lay[kind, l, :cells, hi:rows], spot + width, 1), lay_t)
            lay_b = jnp.where(here, rolled(lay[kind, l, :cells, :LANES], spot, 1), lay_b)
    bottom[:, :LANES] = base_b
    bottom[:, LANES:] = lay_b
    r2 = lax.broadcasted_iota(jnp.int32, (LANES, LANES), 0)
    c2 = lax.broadcasted_iota(jnp.int32, (LANES, LANES), 1)
    perm_b = jnp.where(r2 == (c2 ^ (STRIP - 1)), 1.0, 0.0).astype(F32)
    perm_l = jnp.where(r2 == jnp.where(c2 < 4 * layers, c2 ^ 1, c2), 1.0, 0.0).astype(F32)
    r1 = lax.broadcasted_iota(jnp.int32, (cells, cells), 0)
    c1 = lax.broadcasted_iota(jnp.int32, (cells, cells), 1)
    mirror = jnp.where(r1 + c1 == cells - 1, 1.0, 0.0).astype(F32)
    dot = functools.partial(
        jnp.dot, preferred_element_type=F32, precision=lax.Precision.HIGHEST
    )
    north_edge = c == 1
    top[:, :LANES] = jnp.where(north_edge, dot(mirror, dot(base_t, perm_b)), base_t)
    top[:, LANES:] = jnp.where(north_edge, dot(mirror, dot(lay_t, perm_l)), lay_t)

    far_copies = [
        copy(top, north_ref.at[slot], 4 + slot, target, c)
        for target, slot in zip(far, (OWN, EAST, WEST))
    ]
    up_copies = [
        copy(top, south_ref.at[slot], 7 + slot, target, other)
        for target, slot in zip((z, w, e), (OWN, EAST, WEST))
    ]
    down_copies = [
        copy(bottom, north_ref.at[slot], 10 + slot, target, other)
        for target, slot in zip((z, w, e), (OWN, EAST, WEST))
    ]

    @pl.when(c == 0)
    def _():
        for cp in up_copies:
            cp.start()

    @pl.when(c == 1)
    def _():
        for cp in down_copies:
            cp.start()

    for cp in column_copies:
        cp.start()

    @pl.when(c == 0)
    def _():
        south_ref[...] = jnp.zeros_like(south_ref)
        pl.semaphore_wait(barrier, 3)
        pl.semaphore_signal(
            far_ok, inc=1, device_id={"zonal": z, "merid": other}, device_id_type=MESH
        )

    @pl.when(c == 1)
    def _():
        pl.semaphore_wait(far_ok, 1)

    for target, cp, slot in zip(far, far_copies, (OWN, EAST, WEST)):
        @pl.when(jnp.logical_and(c == 1, target != z))
        def _(cp=cp):
            cp.start()

        @pl.when(jnp.logical_and(c == 1, target == z))
        def _(slot=slot):
            north_ref[slot] = top[...]

    for kind in (H, U, V):
        for l in range(layers):
            lay[kind, l, cells:, :rows] = jnp.zeros((8, rows), F32)

    for cp in side_copies:
        cp.wait()

    @pl.when(c == 0)
    def _():
        for cp in up_copies:
            cp.wait_send()
        for cp in down_copies:
            cp.wait_recv()

    @pl.when(c == 1)
    def _():
        for cp in down_copies:
            cp.wait_send()
        for cp in up_copies:
            cp.wait_recv()

    for target, cp in zip(far, far_copies):
        @pl.when(jnp.logical_and(c == 1, target != z))
        def _(cp=cp):
            cp.wait()

    for k in range(4):
        from_w = inw[k]
        from_e = ine[k]
        base[2 * k, 24:32, :rows] = jnp.where(low4, from_e, from_w)
        if 2 * k + 1 < 7:
            base[2 * k + 1, 24:32, :rows] = pltpu.roll(jnp.where(low4, from_w, from_e), 4, 0)
    first8 = lane_iota((8, LANES)) < LANES // 2
    far_rows = lax.broadcasted_iota(jnp.int32, (8, LANES), 0) < 4
    norths = [north_ref[s, :, :LANES] for s in range(3)]
    souths = [south_ref[s, :, :LANES] for s in range(3)]

    def ring(x):
        outer = jnp.where(far_rows, x[EAST][8:], x[WEST][:8])
        return (x[OWN][:8], x[OWN][8:], x[EAST][:8], outer, x[WEST][8:])

    for k, (n, s) in enumerate(zip(ring(norths), ring(souths))):
        for f in range(7):
            base[f, 8 * k: 8 * k + 8, rows:] = jnp.where(
                first8, rolled(n, -STRIP * f, 1), rolled(s, LANES - STRIP - STRIP * f, 1)
            )
    at_east, at_west, at_south, at_north = neighbours(rows)
    near = lax.broadcasted_iota(jnp.int32, (8, wide), 0) < 4

    def trimmed(x):
        size = x.shape[0]
        return jnp.concatenate([x[:cells], jnp.where(near, x[cells: cells + 8], x[size - 8:])], 0)

    faces_out[0] = trimmed(base[0])
    faces_out[1] = trimmed(base[1])

    def substep(narrow):
        def get(f):
            if narrow:
                return jnp.concatenate([base[f, :cells + 8], base[f, cells + 16:]], 0)
            return base[f]

        def put(f, x):
            if narrow:
                base[f, :cells + 8] = x[:cells + 8]
                base[f, cells + 16:] = x[cells + 8:]
            else:
                base[f] = x

        def run(_, sums):
            sum_u, sum_v = sums
            bu = get(5)
            bv = get(6)
            eta = get(4) - (bu - at_west(bu) + bv - at_south(bv))
            put(4, eta)
            au = get(0)
            bu = jnp.where(au != 0.0, bu - au * (at_east(eta) - eta) + get(2), 0.0)
            put(5, bu)
            av = get(1)
            bv = jnp.where(av != 0.0, bv - av * (at_north(eta) - eta) + get(3), 0.0)
            put(6, bv)
            return sum_u + trimmed(bu), sum_v + trimmed(bv)

        return run

    outer_steps = 2 * NSUB - 8
    zero = jnp.zeros((ext, wide), F32)
    for step in range(STEPS):
        sums = (zero, zero)
        if step == 0:
            sums = lax.fori_loop(0, outer_steps, substep(False), sums)
            sums = lax.fori_loop(outer_steps, NSUB, substep(True), sums)
        else:
            sums = lax.fori_loop(0, NSUB, substep(True), sums)
        means[step, 0] = sums[0] * (1.0 / NSUB)
        means[step, 1] = sums[1] * (1.0 / NSUB)
    for k in range(3):
        state_out[k] = base[4 + k, :cells, :rows]

    def around(x):
        return jnp.concatenate([x[OWN], jnp.where(far_rows, x[EAST][:8], x[WEST][cells - 8:])], 0)

    north = around([north_ref[s, :, LANES:] for s in range(3)])
    south = around([south_ref[s, :, LANES:] for s in range(3)])
    first24 = lane_iota(north.shape) < LANES // 2
    for kind, start, width in ((H, 0, 2), (U, 4 * layers, 1), (V, 2 * layers, 2)):
        for l in range(layers):
            spot = start + width * l
            lay[kind, l, :, rows:] = jnp.where(
                first24, rolled(north, -spot, 1), rolled(south, LANES - width - spot, 1)
            )
    for cp in column_copies:
        cp.wait()
    for kind, east_cols, west_cols in ((H, (0, 1), (0, 1)), (U, (2,), (2, 3)), (V, (3,), (4,))):
        for l in range(layers):
            for k, src in enumerate(east_cols):
                lay[kind, l, cells + k: cells + k + 1, :rows] = least[src * layers + l: src * layers + l + 1, :]
            for k, src in enumerate(west_cols):
                lay[kind, l, ext - 1 - k: ext - k, :rows] = lwest[src * layers + l: src * layers + l + 1, :]


def advance(
    lay_in, means, faces, state, eta_out, bu_out, bv_out, h_out, u_out, v_out,
    lay, trial, results, done,
):
    layers, cells, rows = h_out.shape
    wide = rows + LANES
    ext = cells + 8
    H, U, V = 0, 1, 2
    at_east, at_west, at_south, at_north = neighbours(rows)
    stores = [
        pltpu.make_async_copy(state.at[k], out, done.at[k])
        for k, out in enumerate((eta_out, bu_out, bv_out))
    ] + [
        pltpu.make_async_copy(results.at[k], out, done.at[3 + k])
        for k, out in enumerate((h_out, u_out, v_out))
    ]
    for cp in stores[:3]:
        cp.start()
    zero = jnp.zeros((ext, wide), F32)
    depth_u = None
    depth_v = None
    for outer in range(STEPS):
        source = lay_in if outer == 0 else lay
        press_u = zero
        press_v = zero
        deep_u = zero
        deep_v = zero
        total_u = zero
        total_v = zero
        for l in range(layers):
            h = source[H, l]
            u = source[U, l]
            v = source[V, l]
            diff_u = at_east(h) - h
            diff_v = at_north(h) - h
            press_u = press_u + diff_u
            press_v = press_v + diff_v
            hu = h + 0.5 * diff_u
            hv = h + 0.5 * diff_v
            flux_u = u * hu
            flux_v = v * hv
            new = h - FLUX_STEP * (flux_u - at_west(flux_u) + flux_v - at_south(flux_v))
            if outer == STEPS - 1:
                results[0, l] = new[:cells, :rows]
            else:
                lay[H, l] = new
            ut = u - PRESS_COEF * press_u
            vt = v - PRESS_COEF * press_v
            trial[0, l] = ut
            trial[1, l] = vt
            total_u = total_u + hu * ut
            total_v = total_v + hv * vt
            if outer == 0:
                deep_u = deep_u + hu
                deep_v = deep_v + hv
        if outer == 0:
            depth_u, depth_v = deep_u, deep_v
        if outer == STEPS - 1:
            stores[3].start()
        fix_u = (means[outer, 0] - total_u) / depth_u
        fix_v = (means[outer, 1] - total_v) / depth_v
        for k, fix in ((U, fix_u), (V, fix_v)):
            open_face = faces[k - 1] != 0.0
            for l in range(layers):
                new = jnp.where(open_face, trial[k - 1, l] + fix, 0.0)
                if outer == STEPS - 1:
                    results[k, l] = new[:cells, :rows]
                else:
                    lay[k, l] = new
            if outer == STEPS - 1:
                stores[3 + k].start()
    for cp in stores:
        cp.wait()


def body(
    devices, height, transport_u, transport_v, thickness, velocity_u, velocity_v,
    sea_faces, wind_seeds, wind_scale, wind_base,
):
    layers, cells, rows = thickness.shape
    wide = rows + LANES
    ext = cells + 8
    anywhere = pl.BlockSpec(memory_space=pl.ANY)
    vmem = pl.BlockSpec(memory_space=pltpu.VMEM)

    def shape(*dims):
        return jax.ShapeDtypeStruct(dims, F32)

    def inner(*dims):
        return pltpu.VMEM(dims, F32)

    mid = pl.pallas_call(
        functools.partial(exchange, devices),
        out_shape=[
            inner(3, layers, ext, wide), inner(STEPS, 2, ext, wide), inner(2, ext, wide),
            inner(3, cells, rows),
        ],
        in_specs=[anywhere] * 10,
        out_specs=[vmem] * 4,
        scratch_shapes=[
            inner(7, cells + 24, wide),
            pltpu.VMEM(sea_faces.shape, sea_faces.dtype),
            inner(*wind_base.shape),
            pltpu.SMEM(wind_seeds.shape[::-1], wind_seeds.dtype),
            pltpu.SMEM(wind_scale.shape, F32),
            inner(72, rows), inner(56, rows), inner(56, rows), inner(72, rows),
            inner(4, 8, rows), inner(4, 8, rows), inner(4, 8, rows), inner(4, 8, rows),
            inner(cells, 2 * LANES), inner(cells, 2 * LANES),
            inner(3, cells, 2 * LANES), inner(3, cells, 2 * LANES),
            pltpu.SemaphoreType.DMA((10,)),
            pltpu.SemaphoreType.DMA((15,)),
            pltpu.SemaphoreType.DMA((15,)),
            pltpu.SemaphoreType.REGULAR,
            pltpu.SemaphoreType.REGULAR,
        ],
        compiler_params=pltpu.CompilerParams(collective_id=0, has_side_effects=True),
        name="exchange",
    )(
        height, transport_u, transport_v, thickness, velocity_u, velocity_v,
        sea_faces, wind_base, wind_seeds.T, wind_scale,
    )
    return pl.pallas_call(
        advance,
        out_shape=[shape(cells, rows)] * 3 + [shape(layers, cells, rows)] * 3,
        in_specs=[vmem] * 4,
        out_specs=[anywhere] * 6,
        scratch_shapes=[
            inner(3, layers, ext, wide),
            inner(2, layers, ext, wide),
            inner(3, layers, cells, rows),
            pltpu.SemaphoreType.DMA((6,)),
        ],
        name="advance",
    )(*[pltpu.with_memory_space_constraint(x, pltpu.VMEM) for x in mid])


def solution(mesh):
    flat = P(("members", "zonal"), "merid")
    deep = P(None, ("members", "zonal"), "merid")
    fixed = P(None, "zonal", "merid")
    return jax.shard_map(
        functools.partial(body, mesh.shape["zonal"]),
        mesh=mesh,
        in_specs=(flat, flat, flat, deep, deep, deep, fixed, P("members", None), P("members"), fixed),
        out_specs=(flat, flat, flat, deep, deep, deep),
        check_vma=False,
    )
```

time: 52.2 us -> 42.3 us (0.81)
  Pallas kernels: 50 us -> 41.5 us
  local copies, waits for them, and re-layouts: 1.34 us -> 0 us
    pallas_call x1, Pallas kernels: 8.8 us -> 3.7 us  [body(): pl.pallas_call(advance, out_shape=[shape(cells, rows)] * 3 + [shape(layer...]
    pallas_call x1, Pallas kernels: 41.2 us -> 37.8 us  [body(): pl.pallas_call(functools.partial(exchange, devices), out_shape=[inner(3,...]
    unnamed x1 -> x0, local copies, waits for them, and re-layouts: 1.34 us -> none
where the time goes in v2:
time: 42.3 us; the launch traced here: 42.1 us
  Pallas kernels  41.5 us (98%)
  between operations  0.64 us (2%)
    pallas_call x1, Pallas kernels, body(): pl.pallas_call(functools.partial(exchange, devices), out_shape=[inner(3,...  37.8 us
    pallas_call x1, Pallas kernels, body(): pl.pallas_call(advance, out_shape=[shape(cells, rows)] * 3 + [shape(layer...  3.7 us

profile of v2, /device:TPU:37, one launch (start us, length us, event | category | flops | bytes accessed | tf_op | source)
XLA Modules:
  0.0 42.1 jit_solution(9273983465914592347)
XLA Ops:
  0.6 37.8 %exchange.1 = (f32[3,14,24,640]{3,2,1,0:T(8,128)S(1)}, f32[2,2,24,640]{3,2,1,0:T(8,128)S(1)}, f32[2,24,640]{2,1,0:T(8,128)S(1)}, f32[3,16,512]{2,1,0:T(8,128)S(1)}) custom-call(f32[16,512]{1,0:T(8,128)} %eta_ref.1, f32[16,512]{1,0:T(8,128)} %bu_ref.1, f32[16,512]{1,0:T(8,128)} %bv_ref.1, f32[14,16,512]{2,1,0:T(8,128)} %h_ref.1, f32[14,16,512]{2,1,0:T(8,128)} %u_ref.1, ...), custom_call_target="tpu_custom_call" | custom-call | tf_op jit(solution)/shard_map/exchange/pallas_call | solution.py:484
  38.4 3.7 %advance.1 = (f32[16,512]{1,0:T(8,128)}, f32[16,512]{1,0:T(8,128)}, f32[16,512]{1,0:T(8,128)}, f32[14,16,512]{2,1,0:T(8,128)}, f32[14,16,512]{2,1,0:T(8,128)}, /*index=5*/f32[14,16,512]{2,1,0:T(8,128)}) custom-call(f32[3,14,24,640]{3,2,1,0:T(8,128)S(1)} %get-tuple-element.10.lay_in, f32[2,2,24,640]{3,2,1,0:T(8,128)S(1)} %get-tuple-element.11.means, ...), custom_call_target="tpu_custom_call" | custom-call | tf_op jit(solution)/shard_map/advance/pallas_call | solution.py:514

commit v3 on v2

--- a/solution.py
+++ b/solution.py
@@ -63,8 +63,8 @@
     eta_ref, bu_ref, bv_ref, h_ref, u_ref, v_ref, faces_ref, base_ref, seeds_ref, scale_ref,
     lay, means, faces_out, state_out,
     base, faces, winds, seeds, scale, goeast, gowest, least, lwest, outw, oute, inw, ine,
-    top, bottom, north_ref, south_ref,
-    load, send, recv, near_ok, far_ok,
+    top, bottom, top_side, bottom_side, north_ref, south_ref, north_side, south_side,
+    load, send, recv, near_ok, west_ok, far_ok,
 ):
     z = lax.axis_index("zonal")
     c = lax.axis_index("merid")
@@ -77,43 +77,86 @@
     ext = cells + 8
     H, U, V = 0, 1, 2
 
-    barrier = pltpu.get_barrier_semaphore()
-
-    def greet(zonal, merid):
-        pl.semaphore_signal(
-            barrier, inc=1, device_id={"zonal": zonal, "merid": merid}, device_id_type=MESH
-        )
-
-    greet(e, 1)
-    greet(w, 1)
-
-    @pl.when(c == 0)
-    def _():
-        greet(z, 1)
-
-    @pl.when(c == 1)
-    def _():
-        for target in far:
-            greet(target, 0)
-
     fetches = [
         pltpu.make_async_copy(src, dst, load.at[k])
         for k, (src, dst) in enumerate((
-            (h_ref, lay.at[H, :, pl.ds(0, cells), pl.ds(0, rows)]),
+            (eta_ref, base.at[4, pl.ds(0, cells), pl.ds(0, rows)]),
+            (bu_ref, base.at[5, pl.ds(0, cells), pl.ds(0, rows)]),
+            (bv_ref, base.at[6, pl.ds(0, cells), pl.ds(0, rows)]),
             (seeds_ref, seeds),
             (scale_ref, scale),
             (faces_ref, faces),
             (base_ref, winds),
-            (eta_ref, base.at[4, pl.ds(0, cells), pl.ds(0, rows)]),
-            (bu_ref, base.at[5, pl.ds(0, cells), pl.ds(0, rows)]),
-            (bv_ref, base.at[6, pl.ds(0, cells), pl.ds(0, rows)]),
+            (h_ref, lay.at[H, :, pl.ds(0, cells), pl.ds(0, rows)]),
             (u_ref, lay.at[U, :, pl.ds(0, cells), pl.ds(0, rows)]),
             (v_ref, lay.at[V, :, pl.ds(0, cells), pl.ds(0, rows)]),
         ))
     ]
     for cp in fetches:
         cp.start()
-    for cp in fetches[1:5]:
+    barrier = pltpu.get_barrier_semaphore()
+
+    def greet(zonal, merid):
+        pl.semaphore_signal(
+            barrier, inc=1, device_id={"zonal": zonal, "merid": merid}, device_id_type=MESH
+        )
+
+    greet(w, 1)
+
+    @pl.when(c == 0)
+    def _():
+        greet(z, 1)
+
+    @pl.when(c == 1)
+    def _():
+        for target in far:
+            greet(target, 0)
+
+    def copy(src, dst, k, zonal, merid):
+        return pltpu.make_async_remote_copy(
+            src_ref=src, dst_ref=dst, send_sem=send.at[k], recv_sem=recv.at[k],
+            device_id={"zonal": zonal, "merid": merid}, device_id_type=MESH,
+        )
+
+    lanes = pl.ds(0, rows)
+
+    def to_sides(fields, k):
+        return [
+            copy(base.at[fields, pl.ds(8, 8), lanes], base.at[fields, pl.ds(32, 8), lanes], k, e, c),
+            copy(base.at[fields, pl.ds(0, 8), lanes], base.at[fields, pl.ds(16, 8), lanes], k + 1, w, c),
+        ]
+
+    state_copies = to_sides(pl.ds(4, 3), 15)
+    side_copies = to_sides(pl.ds(0, 4), 0) + [
+        copy(oute, inw, 2, e, c),
+        copy(outw, ine, 3, w, c),
+    ]
+    column_copies = [
+        copy(goeast, lwest, 13, e, c),
+        copy(gowest, least, 14, w, c),
+    ]
+
+    for cp in fetches[:3]:
+        cp.wait()
+
+    def tell(semaphore, zonal, merid):
+        pl.semaphore_signal(
+            semaphore, inc=1, device_id={"zonal": zonal, "merid": merid}, device_id_type=MESH
+        )
+
+    @pl.when(c == 1)
+    def _():
+        pl.semaphore_wait(barrier, 3)
+        tell(near_ok, z, other)
+        tell(west_ok, e, 1)
+        tell(west_ok, e, 0)
+
+    @pl.when(c == 0)
+    def _():
+        pl.semaphore_wait(near_ok, 1)
+
+    state_copies[0].start()
+    for cp in fetches[3:7]:
         cp.wait()
     total_x = cells * devices
     total_y = rows * 2
@@ -135,14 +178,14 @@
     mask_v = faces[1].astype(F32)
     base[2, :cells, :rows] = mask_u * (STRESS_SCALE * (winds[0] + sum_cos))
     base[3, :cells, :rows] = mask_v * (STRESS_SCALE * (winds[1] + sum_sin))
-    fetches[0].wait()
+    fetches[7].wait()
     h_sum = lay[H, 0, :cells, :rows]
     for l in range(1, layers):
         h_sum = h_sum + lay[H, l, :cells, :rows]
     wave = (WAVE_LIMIT / layers) * h_sum
     base[0, :cells, :rows] = mask_u * wave
     base[1, :cells, :rows] = mask_v * wave
-    for cp in fetches[5:]:
+    for cp in fetches[8:]:
         cp.wait()
     low4 = lax.broadcasted_iota(jnp.int32, (8, rows), 0) < 4
     for k in range(4):
@@ -154,42 +197,18 @@
         oute[k] = a
         outw[k] = b
     last = cells - 1
-    for k, (kind, col) in enumerate(((H, last), (H, last - 1), (U, last), (U, last - 1), (V, last))):
-        goeast[k * layers: (k + 1) * layers] = lay[kind, :, col, :rows]
-    for k, (kind, col) in enumerate(((H, 0), (H, 1), (U, 0), (V, 0))):
-        gowest[k * layers: (k + 1) * layers] = lay[kind, :, col, :rows]
-
-    def copy(src, dst, k, zonal, merid):
-        return pltpu.make_async_remote_copy(
-            src_ref=src, dst_ref=dst, send_sem=send.at[k], recv_sem=recv.at[k],
-            device_id={"zonal": zonal, "merid": merid}, device_id_type=MESH,
-        )
-
-    lanes = pl.ds(0, rows)
-    side_copies = [
-        copy(base.at[:, pl.ds(8, 8), lanes], base.at[:, pl.ds(32, 8), lanes], 0, e, c),
-        copy(base.at[:, pl.ds(0, 8), lanes], base.at[:, pl.ds(16, 8), lanes], 1, w, c),
-        copy(oute, inw, 2, e, c),
-        copy(outw, ine, 3, w, c),
-    ]
-    column_copies = [
-        copy(goeast, lwest, 13, e, c),
-        copy(gowest, least, 14, w, c),
-    ]
-
-    @pl.when(c == 1)
-    def _():
-        pl.semaphore_wait(barrier, 5)
-        pl.semaphore_signal(
-            near_ok, inc=1, device_id={"zonal": z, "merid": other}, device_id_type=MESH
-        )
-
-    @pl.when(c == 0)
-    def _():
-        pl.semaphore_wait(near_ok, 1)
-
-    for cp in side_copies:
-        cp.start()
+    h_last = lay[H, :, last, :rows]
+    u_last = lay[U, :, last, :rows]
+    flux_in = lay[U, :, last - 1, :rows] * (0.5 * (lay[H, :, last - 1, :rows] + h_last))
+    for k, x in enumerate((h_last, u_last, flux_in, lay[V, :, last, :rows])):
+        goeast[k * layers: (k + 1) * layers] = x
+    h_first = lay[H, :, 0, :rows]
+    flux_out = lay[U, :, 0, :rows] * (0.5 * (h_first + lay[H, :, 1, :rows]))
+    for k, x in enumerate((h_first, flux_out, lay[V, :, 0, :rows])):
+        gowest[k * layers: (k + 1) * layers] = x
+
+    side_copies[0].start()
+    side_copies[2].start()
     lane = lane_iota((cells, LANES))
     hi = rows - LANES
     base_t = jnp.zeros((cells, LANES), F32)
@@ -206,8 +225,6 @@
             here = jnp.logical_and(lane >= spot, lane < spot + width)
             lay_t = jnp.where(here, rolled(lay[kind, l, :cells, hi:rows], spot + width, 1), lay_t)
             lay_b = jnp.where(here, rolled(lay[kind, l, :cells, :LANES], spot, 1), lay_b)
-    bottom[:, :LANES] = base_b
-    bottom[:, LANES:] = lay_b
     r2 = lax.broadcasted_iota(jnp.int32, (LANES, LANES), 0)
     c2 = lax.broadcasted_iota(jnp.int32, (LANES, LANES), 1)
     perm_b = jnp.where(r2 == (c2 ^ (STRIP - 1)), 1.0, 0.0).astype(F32)
@@ -219,61 +236,101 @@
         jnp.dot, preferred_element_type=F32, precision=lax.Precision.HIGHEST
     )
     north_edge = c == 1
-    top[:, :LANES] = jnp.where(north_edge, dot(mirror, dot(base_t, perm_b)), base_t)
-    top[:, LANES:] = jnp.where(north_edge, dot(mirror, dot(lay_t, perm_l)), lay_t)
-
-    far_copies = [
-        copy(top, north_ref.at[slot], 4 + slot, target, c)
-        for target, slot in zip(far, (OWN, EAST, WEST))
-    ]
-    up_copies = [
-        copy(top, south_ref.at[slot], 7 + slot, target, other)
-        for target, slot in zip((z, w, e), (OWN, EAST, WEST))
-    ]
-    down_copies = [
-        copy(bottom, north_ref.at[slot], 10 + slot, target, other)
-        for target, slot in zip((z, w, e), (OWN, EAST, WEST))
-    ]
+    base_t = jnp.where(north_edge, dot(mirror, dot(base_t, perm_b)), base_t)
+    lay_t = jnp.where(north_edge, dot(mirror, dot(lay_t, perm_l)), lay_t)
+    sub = lax.broadcasted_iota(jnp.int32, (8, LANES), 0)
+    for whole, side, fields, columns in ((top, top_side, base_t, lay_t), (bottom, bottom_side, base_b, lay_b)):
+        whole[:, :LANES] = fields
+        whole[:, LANES:] = columns
+        side[0, 0:8] = jnp.where(sub < 2, pltpu.roll(columns[8:], 2, 0), fields[:8])
+        side[0, 8:16] = fields[8:]
+        side[1, 0:8] = fields[:8]
+        side[1, 8:16] = jnp.where(sub >= 6, pltpu.roll(columns[:8], 6, 0), fields[8:])
+
+    def strips(whole, side, into, into_side, k, own, to_west_slot, to_east_slot, merid):
+        return [
+            copy(whole, into, k, own, merid),
+            copy(side.at[0], into_side.at[0], k + 1, to_west_slot, merid),
+            copy(side.at[1], into_side.at[1], k + 2, to_east_slot, merid),
+        ]
+
+    far_targets = (far[0], far[2], far[1])
+    far_copies = strips(top, top_side, north_ref, north_side, 4, *far_targets, c)
+    up_copies = strips(top, top_side, south_ref, south_side, 7, z, e, w, other)
+    down_copies = strips(bottom, bottom_side, north_ref, north_side, 10, z, e, w, other)
 
     @pl.when(c == 0)
     def _():
-        for cp in up_copies:
-            cp.start()
+        up_copies[0].start()
+        up_copies[1].start()
 
     @pl.when(c == 1)
     def _():
-        for cp in down_copies:
-            cp.start()
-
-    for cp in column_copies:
-        cp.start()
+        down_copies[0].start()
+        down_copies[1].start()
+
+    def send_far():
+        @pl.when(c == 0)
+        def _():
+            pl.semaphore_wait(barrier, 3)
+            pl.semaphore_signal(
+                far_ok, inc=1, device_id={"zonal": z, "merid": other}, device_id_type=MESH
+            )
+
+        @pl.when(c == 1)
+        def _():
+            pl.semaphore_wait(far_ok, 1)
+            for target, cp in zip(far_targets, far_copies):
+                @pl.when(target != z)
+                def _(cp=cp):
+                    cp.start()
+
+    late = 2 * z >= devices
+
+    @pl.when(late)
+    def _():
+        send_far()
+
+    column_copies[0].start()
+
+    pl.semaphore_wait(west_ok, 1)
+    state_copies[1].start()
+    side_copies[1].start()
+    side_copies[3].start()
 
     @pl.when(c == 0)
     def _():
+        up_copies[2].start()
+
+    @pl.when(c == 1)
+    def _():
+        down_copies[2].start()
+
+    column_copies[1].start()
+
+    @pl.when(jnp.logical_not(late))
+    def _():
+        send_far()
+
+    @pl.when(c == 0)
+    def _():
         south_ref[...] = jnp.zeros_like(south_ref)
-        pl.semaphore_wait(barrier, 3)
-        pl.semaphore_signal(
-            far_ok, inc=1, device_id={"zonal": z, "merid": other}, device_id_type=MESH
-        )
-
-    @pl.when(c == 1)
-    def _():
-        pl.semaphore_wait(far_ok, 1)
-
-    for target, cp, slot in zip(far, far_copies, (OWN, EAST, WEST)):
-        @pl.when(jnp.logical_and(c == 1, target != z))
-        def _(cp=cp):
-            cp.start()
-
+        south_side[...] = jnp.zeros_like(south_side)
+
+    for target, dst, src in (
+        (far_targets[0], north_ref, top),
+        (far_targets[1], north_side.at[0], top_side.at[0]),
+        (far_targets[2], north_side.at[1], top_side.at[1]),
+    ):
         @pl.when(jnp.logical_and(c == 1, target == z))
-        def _(slot=slot):
-            north_ref[slot] = top[...]
+        def _(dst=dst, src=src):
+            dst[...] = src[...]
 
     for kind in (H, U, V):
         for l in range(layers):
             lay[kind, l, cells:, :rows] = jnp.zeros((8, rows), F32)
 
-    for cp in side_copies:
+    for cp in state_copies + side_copies:
         cp.wait()
 
     @pl.when(c == 0)
@@ -290,7 +347,7 @@
         for cp in up_copies:
             cp.wait_recv()
 
-    for target, cp in zip(far, far_copies):
+    for target, cp in zip(far_targets, far_copies):
         @pl.when(jnp.logical_and(c == 1, target != z))
         def _(cp=cp):
             cp.wait()
@@ -303,8 +360,8 @@
             base[2 * k + 1, 24:32, :rows] = pltpu.roll(jnp.where(low4, from_w, from_e), 4, 0)
     first8 = lane_iota((8, LANES)) < LANES // 2
     far_rows = lax.broadcasted_iota(jnp.int32, (8, LANES), 0) < 4
-    norths = [north_ref[s, :, :LANES] for s in range(3)]
-    souths = [south_ref[s, :, :LANES] for s in range(3)]
+    norths = [north_ref[:, :LANES], north_side[1], north_side[0]]
+    souths = [south_ref[:, :LANES], south_side[1], south_side[0]]
 
     def ring(x):
         outer = jnp.where(far_rows, x[EAST][8:], x[WEST][:8])
@@ -368,11 +425,12 @@
     for k in range(3):
         state_out[k] = base[4 + k, :cells, :rows]
 
-    def around(x):
-        return jnp.concatenate([x[OWN], jnp.where(far_rows, x[EAST][:8], x[WEST][cells - 8:])], 0)
-
-    north = around([north_ref[s, :, LANES:] for s in range(3)])
-    south = around([south_ref[s, :, LANES:] for s in range(3)])
+    def around(own, sides):
+        halo = jnp.where(far_rows, pltpu.roll(sides[1, 8:], 2, 0), pltpu.roll(sides[0, :8], 6, 0))
+        return jnp.concatenate([own[:, LANES:], halo], 0)
+
+    north = around(north_ref, north_side)
+    south = around(south_ref, south_side)
     first24 = lane_iota(north.shape) < LANES // 2
     for kind, start, width in ((H, 0, 2), (U, 4 * layers, 1), (V, 2 * layers, 2)):
         for l in range(layers):
@@ -382,17 +440,24 @@
             )
     for cp in column_copies:
         cp.wait()
-    for kind, east_cols, west_cols in ((H, (0, 1), (0, 1)), (U, (2,), (2, 3)), (V, (3,), (4,))):
-        for l in range(layers):
-            for k, src in enumerate(east_cols):
-                lay[kind, l, cells + k: cells + k + 1, :rows] = least[src * layers + l: src * layers + l + 1, :]
-            for k, src in enumerate(west_cols):
-                lay[kind, l, ext - 1 - k: ext - k, :rows] = lwest[src * layers + l: src * layers + l + 1, :]
+    for l in range(layers):
+        def column(ref, k):
+            return ref[k * layers + l: k * layers + l + 1, :]
+
+        lay[H, l, cells: cells + 1, :rows] = column(least, 0)
+        lay[H, l, cells + 1: cells + 2, :rows] = 2.0 - column(least, 0)
+        lay[U, l, cells: cells + 1, :rows] = column(least, 1)
+        lay[V, l, cells: cells + 1, :rows] = column(least, 2)
+        lay[H, l, ext - 1: ext, :rows] = column(lwest, 0)
+        lay[H, l, ext - 2: ext - 1, :rows] = 2.0 - column(lwest, 0)
+        lay[U, l, ext - 1: ext, :rows] = column(lwest, 1)
+        lay[U, l, ext - 2: ext - 1, :rows] = column(lwest, 2)
+        lay[V, l, ext - 1: ext, :rows] = column(lwest, 3)
 
 
 def advance(
     lay_in, means, faces, state, eta_out, bu_out, bv_out, h_out, u_out, v_out,
-    lay, trial, results, done,
+    lay, trial, depth, results, done,
 ):
     layers, cells, rows = h_out.shape
     wide = rows + LANES
@@ -408,58 +473,63 @@
     ]
     for cp in stores[:3]:
         cp.start()
-    zero = jnp.zeros((ext, wide), F32)
-    depth_u = None
-    depth_v = None
     for outer in range(STEPS):
+        final = outer == STEPS - 1
         source = lay_in if outer == 0 else lay
-        press_u = zero
-        press_v = zero
-        deep_u = zero
-        deep_v = zero
-        total_u = zero
-        total_v = zero
+        size_c, size_r = (cells, rows) if final else (ext, wide)
+        press_u = press_v = total_u = total_v = jnp.zeros((size_c, size_r), F32)
+        deep_u = deep_v = press_u
         for l in range(layers):
             h = source[H, l]
             u = source[U, l]
             v = source[V, l]
-            diff_u = at_east(h) - h
-            diff_v = at_north(h) - h
+            if final:
+                diff_u = rolled(h[:, :rows], -1, 0) - h[:, :rows]
+                diff_v = rolled(h[:cells], -1, 1) - h[:cells]
+                hu = h[:, :rows] + 0.5 * diff_u
+                hv = h[:cells] + 0.5 * diff_v
+                flux_u = u[:, :rows] * hu
+                flux_v = v[:cells] * hv
+                out_u = (flux_u - rolled(flux_u, 1, 0))[:cells]
+                out_v = (flux_v - rolled(flux_v, 1, 1))[:, :rows]
+                results[0, l] = h[:cells, :rows] - FLUX_STEP * (out_u + out_v)
+                diff_u, hu = diff_u[:cells], hu[:cells]
+                diff_v, hv = diff_v[:, :rows], hv[:, :rows]
+                u, v = u[:cells, :rows], v[:cells, :rows]
+            else:
+                diff_u = at_east(h) - h
+                diff_v = at_north(h) - h
+                hu = h + 0.5 * diff_u
+                hv = h + 0.5 * diff_v
+                flux_u = u * hu
+                flux_v = v * hv
+                lay[H, l] = h - FLUX_STEP * (flux_u - at_west(flux_u) + flux_v - at_south(flux_v))
             press_u = press_u + diff_u
             press_v = press_v + diff_v
-            hu = h + 0.5 * diff_u
-            hv = h + 0.5 * diff_v
-            flux_u = u * hu
-            flux_v = v * hv
-            new = h - FLUX_STEP * (flux_u - at_west(flux_u) + flux_v - at_south(flux_v))
-            if outer == STEPS - 1:
-                results[0, l] = new[:cells, :rows]
-            else:
-                lay[H, l] = new
             ut = u - PRESS_COEF * press_u
             vt = v - PRESS_COEF * press_v
-            trial[0, l] = ut
-            trial[1, l] = vt
+            trial[0, l, :size_c, :size_r] = ut
+            trial[1, l, :size_c, :size_r] = vt
             total_u = total_u + hu * ut
             total_v = total_v + hv * vt
             if outer == 0:
                 deep_u = deep_u + hu
                 deep_v = deep_v + hv
         if outer == 0:
-            depth_u, depth_v = deep_u, deep_v
-        if outer == STEPS - 1:
+            depth[0] = deep_u
+            depth[1] = deep_v
+        if final:
             stores[3].start()
-        fix_u = (means[outer, 0] - total_u) / depth_u
-        fix_v = (means[outer, 1] - total_v) / depth_v
-        for k, fix in ((U, fix_u), (V, fix_v)):
-            open_face = faces[k - 1] != 0.0
+        for k, total in ((U, total_u), (V, total_v)):
+            fix = (means[outer, k - 1, :size_c, :size_r] - total) / depth[k - 1, :size_c, :size_r]
+            open_face = faces[k - 1, :size_c, :size_r] != 0.0
             for l in range(layers):
-                new = jnp.where(open_face, trial[k - 1, l] + fix, 0.0)
-                if outer == STEPS - 1:
-                    results[k, l] = new[:cells, :rows]
+                new = jnp.where(open_face, trial[k - 1, l, :size_c, :size_r] + fix, 0.0)
+                if final:
+                    results[k, l] = new
                 else:
                     lay[k, l] = new
-            if outer == STEPS - 1:
+            if final:
                 stores[3 + k].start()
     for cp in stores:
         cp.wait()
@@ -495,13 +565,14 @@
             inner(*wind_base.shape),
             pltpu.SMEM(wind_seeds.shape[::-1], wind_seeds.dtype),
             pltpu.SMEM(wind_scale.shape, F32),
-            inner(72, rows), inner(56, rows), inner(56, rows), inner(72, rows),
+            inner(4 * layers, rows), inner(3 * layers, rows), inner(3 * layers, rows), inner(4 * layers, rows),
             inner(4, 8, rows), inner(4, 8, rows), inner(4, 8, rows), inner(4, 8, rows),
-            inner(cells, 2 * LANES), inner(cells, 2 * LANES),
-            inner(3, cells, 2 * LANES), inner(3, cells, 2 * LANES),
+            inner(cells, 2 * LANES), inner(cells, 2 * LANES), inner(2, cells, LANES), inner(2, cells, LANES),
+            inner(cells, 2 * LANES), inner(cells, 2 * LANES), inner(2, cells, LANES), inner(2, cells, LANES),
             pltpu.SemaphoreType.DMA((10,)),
-            pltpu.SemaphoreType.DMA((15,)),
-            pltpu.SemaphoreType.DMA((15,)),
+            pltpu.SemaphoreType.DMA((17,)),
+            pltpu.SemaphoreType.DMA((17,)),
+            pltpu.SemaphoreType.REGULAR,
             pltpu.SemaphoreType.REGULAR,
             pltpu.SemaphoreType.REGULAR,
         ],
@@ -519,6 +590,7 @@
         scratch_shapes=[
             inner(3, layers, ext, wide),
             inner(2, layers, ext, wide),
+            inner(2, ext, wide),
             inner(3, layers, cells, rows),
             pltpu.SemaphoreType.DMA((6,)),
         ],

time: 42.3 us -> 40 us (0.946)
  Pallas kernels: 41.5 us -> 39.2 us
    pallas_call x1, Pallas kernels: 37.8 us -> 35.6 us  [body(): pl.pallas_call(functools.partial(exchange, devices), out_shape=[inner(3,...]
where the time goes in v3:
time: 40 us; the launch traced here: 39.8 us
  Pallas kernels  39.2 us (98%)
  between operations  0.64 us (2%)
    pallas_call x1, Pallas kernels, body(): pl.pallas_call(functools.partial(exchange, devices), out_shape=[inner(3,...  35.6 us
    pallas_call x1, Pallas kernels, body(): pl.pallas_call(advance, out_shape=[shape(cells, rows)] * 3 + [shape(layer...  3.62 us

profile of v3, /device:TPU:37, one launch (start us, length us, event | category | flops | bytes accessed | tf_op | source)
XLA Modules:
  0.0 39.8 jit_solution(1244246305599552919)
XLA Ops:
  0.6 35.6 %exchange.1 = (f32[3,14,24,640]{3,2,1,0:T(8,128)S(1)}, f32[2,2,24,640]{3,2,1,0:T(8,128)S(1)}, f32[2,24,640]{2,1,0:T(8,128)S(1)}, f32[3,16,512]{2,1,0:T(8,128)S(1)}) custom-call(f32[16,512]{1,0:T(8,128)} %eta_ref.1, f32[16,512]{1,0:T(8,128)} %bu_ref.1, f32[16,512]{1,0:T(8,128)} %bv_ref.1, f32[14,16,512]{2,1,0:T(8,128)} %h_ref.1, f32[14,16,512]{2,1,0:T(8,128)} %u_ref.1, ...), custom_call_target="tpu_custom_call" | custom-call | tf_op jit(solution)/shard_map/exchange/pallas_call | solution.py:554
  36.2 3.6 %advance.1 = (f32[16,512]{1,0:T(8,128)}, f32[16,512]{1,0:T(8,128)}, f32[16,512]{1,0:T(8,128)}, f32[14,16,512]{2,1,0:T(8,128)}, f32[14,16,512]{2,1,0:T(8,128)}, /*index=5*/f32[14,16,512]{2,1,0:T(8,128)}) custom-call(f32[3,14,24,640]{3,2,1,0:T(8,128)S(1)} %get-tuple-element.10.lay_in, f32[2,2,24,640]{3,2,1,0:T(8,128)S(1)} %get-tuple-element.11.means, ...), custom_call_target="tpu_custom_call" | custom-call | tf_op jit(solution)/shard_map/advance/pallas_call | solution.py:585

commit v4 on v3

--- a/solution.py
+++ b/solution.py
@@ -61,8 +61,8 @@
 def exchange(
     devices,
     eta_ref, bu_ref, bv_ref, h_ref, u_ref, v_ref, faces_ref, base_ref, seeds_ref, scale_ref,
-    lay, means, faces_out, state_out,
-    base, faces, winds, seeds, scale, goeast, gowest, least, lwest, outw, oute, inw, ine,
+    h_new, trial, fixes, faces_out, state_out,
+    base, lay, halo_trial, depth, faces, winds, seeds, scale, goeast, gowest, least, lwest, late_east, late_west,
     top, bottom, top_side, bottom_side, north_ref, south_ref, north_side, south_side,
     load, send, recv, near_ok, west_ok, far_ok,
 ):
@@ -122,14 +122,15 @@
 
     def to_sides(fields, k):
         return [
-            copy(base.at[fields, pl.ds(8, 8), lanes], base.at[fields, pl.ds(32, 8), lanes], k, e, c),
+            copy(base.at[fields, pl.ds(8, 8), lanes], base.at[fields, pl.ds(24, 8), lanes], k, e, c),
             copy(base.at[fields, pl.ds(0, 8), lanes], base.at[fields, pl.ds(16, 8), lanes], k + 1, w, c),
         ]
 
     state_copies = to_sides(pl.ds(4, 3), 15)
-    side_copies = to_sides(pl.ds(0, 4), 0) + [
-        copy(oute, inw, 2, e, c),
-        copy(outw, ine, 3, w, c),
+    side_copies = to_sides(pl.ds(0, 4), 0)
+    second_copies = [
+        copy(base.at[pl.ds(4, 3), pl.ds(8, 8)], late_west, 2, e, c),
+        copy(base.at[pl.ds(4, 3), pl.ds(0, 8)], late_east, 3, w, c),
     ]
     column_copies = [
         copy(goeast, lwest, 13, e, c),
@@ -187,15 +188,6 @@
     base[1, :cells, :rows] = mask_v * wave
     for cp in fetches[8:]:
         cp.wait()
-    low4 = lax.broadcasted_iota(jnp.int32, (8, rows), 0) < 4
-    for k in range(4):
-        a = base[2 * k, 0:8, :rows]
-        b = base[2 * k, 8:16, :rows]
-        if 2 * k + 1 < 7:
-            a = jnp.where(low4, pltpu.roll(base[2 * k + 1, 0:8, :rows], 4, 0), a)
-            b = jnp.where(low4, b, pltpu.roll(base[2 * k + 1, 8:16, :rows], 4, 0))
-        oute[k] = a
-        outw[k] = b
     last = cells - 1
     h_last = lay[H, :, last, :rows]
     u_last = lay[U, :, last, :rows]
@@ -208,7 +200,6 @@
         gowest[k * layers: (k + 1) * layers] = x
 
     side_copies[0].start()
-    side_copies[2].start()
     lane = lane_iota((cells, LANES))
     hi = rows - LANES
     base_t = jnp.zeros((cells, LANES), F32)
@@ -296,7 +287,6 @@
     pl.semaphore_wait(west_ok, 1)
     state_copies[1].start()
     side_copies[1].start()
-    side_copies[3].start()
 
     @pl.when(c == 0)
     def _():
@@ -352,20 +342,13 @@
         def _(cp=cp):
             cp.wait()
 
-    for k in range(4):
-        from_w = inw[k]
-        from_e = ine[k]
-        base[2 * k, 24:32, :rows] = jnp.where(low4, from_e, from_w)
-        if 2 * k + 1 < 7:
-            base[2 * k + 1, 24:32, :rows] = pltpu.roll(jnp.where(low4, from_w, from_e), 4, 0)
     first8 = lane_iota((8, LANES)) < LANES // 2
     far_rows = lax.broadcasted_iota(jnp.int32, (8, LANES), 0) < 4
     norths = [north_ref[:, :LANES], north_side[1], north_side[0]]
     souths = [south_ref[:, :LANES], south_side[1], south_side[0]]
 
     def ring(x):
-        outer = jnp.where(far_rows, x[EAST][8:], x[WEST][:8])
-        return (x[OWN][:8], x[OWN][8:], x[EAST][:8], outer, x[WEST][8:])
+        return (x[OWN][:8], x[OWN][8:], x[EAST][:8], x[WEST][8:])
 
     for k, (n, s) in enumerate(zip(ring(norths), ring(souths))):
         for f in range(7):
@@ -376,54 +359,35 @@
     near = lax.broadcasted_iota(jnp.int32, (8, wide), 0) < 4
 
     def trimmed(x):
-        size = x.shape[0]
-        return jnp.concatenate([x[:cells], jnp.where(near, x[cells: cells + 8], x[size - 8:])], 0)
-
-    faces_out[0] = trimmed(base[0])
-    faces_out[1] = trimmed(base[1])
-
-    def substep(narrow):
-        def get(f):
-            if narrow:
-                return jnp.concatenate([base[f, :cells + 8], base[f, cells + 16:]], 0)
-            return base[f]
-
-        def put(f, x):
-            if narrow:
-                base[f, :cells + 8] = x[:cells + 8]
-                base[f, cells + 16:] = x[cells + 8:]
-            else:
-                base[f] = x
-
-        def run(_, sums):
-            sum_u, sum_v = sums
-            bu = get(5)
-            bv = get(6)
-            eta = get(4) - (bu - at_west(bu) + bv - at_south(bv))
-            put(4, eta)
-            au = get(0)
-            bu = jnp.where(au != 0.0, bu - au * (at_east(eta) - eta) + get(2), 0.0)
-            put(5, bu)
-            av = get(1)
-            bv = jnp.where(av != 0.0, bv - av * (at_north(eta) - eta) + get(3), 0.0)
-            put(6, bv)
-            return sum_u + trimmed(bu), sum_v + trimmed(bv)
-
-        return run
-
-    outer_steps = 2 * NSUB - 8
+        return jnp.concatenate([x[:cells], jnp.where(near, x[cells: cells + 8], x[cells + 8:])], 0)
+
+    def move(_):
+        bu = base[5]
+        bv = base[6]
+        eta = base[4] - (bu - at_west(bu) + bv - at_south(bv))
+        base[4] = eta
+        au = base[0]
+        bu = jnp.where(au != 0.0, bu - au * (at_east(eta) - eta) + base[2], 0.0)
+        base[5] = bu
+        av = base[1]
+        bv = jnp.where(av != 0.0, bv - av * (at_north(eta) - eta) + base[3], 0.0)
+        base[6] = bv
+        return bu, bv
+
+    def substep(k, sums):
+        bu, bv = move(k)
+        return sums[0] + trimmed(bu), sums[1] + trimmed(bv)
+
+    def substep_own(k):
+        bu, bv = move(k)
+        return bu[:cells, :rows], bv[:cells, :rows]
+
     zero = jnp.zeros((ext, wide), F32)
-    for step in range(STEPS):
-        sums = (zero, zero)
-        if step == 0:
-            sums = lax.fori_loop(0, outer_steps, substep(False), sums)
-            sums = lax.fori_loop(outer_steps, NSUB, substep(True), sums)
-        else:
-            sums = lax.fori_loop(0, NSUB, substep(True), sums)
-        means[step, 0] = sums[0] * (1.0 / NSUB)
-        means[step, 1] = sums[1] * (1.0 / NSUB)
-    for k in range(3):
-        state_out[k] = base[4 + k, :cells, :rows]
+    mean_u, mean_v = lax.fori_loop(0, NSUB, substep, (zero, zero))
+    for cp in second_copies:
+        cp.start()
+    depth[2] = mean_u * (1.0 / NSUB)
+    depth[3] = mean_v * (1.0 / NSUB)
 
     def around(own, sides):
         halo = jnp.where(far_rows, pltpu.roll(sides[1, 8:], 2, 0), pltpu.roll(sides[0, :8], 6, 0))
@@ -453,36 +417,15 @@
         lay[U, l, ext - 1: ext, :rows] = column(lwest, 1)
         lay[U, l, ext - 2: ext - 1, :rows] = column(lwest, 2)
         lay[V, l, ext - 1: ext, :rows] = column(lwest, 3)
-
-
-def advance(
-    lay_in, means, faces, state, eta_out, bu_out, bv_out, h_out, u_out, v_out,
-    lay, trial, depth, results, done,
-):
-    layers, cells, rows = h_out.shape
-    wide = rows + LANES
-    ext = cells + 8
-    H, U, V = 0, 1, 2
-    at_east, at_west, at_south, at_north = neighbours(rows)
-    stores = [
-        pltpu.make_async_copy(state.at[k], out, done.at[k])
-        for k, out in enumerate((eta_out, bu_out, bv_out))
-    ] + [
-        pltpu.make_async_copy(results.at[k], out, done.at[3 + k])
-        for k, out in enumerate((h_out, u_out, v_out))
-    ]
-    for cp in stores[:3]:
-        cp.start()
     for outer in range(STEPS):
         final = outer == STEPS - 1
-        source = lay_in if outer == 0 else lay
         size_c, size_r = (cells, rows) if final else (ext, wide)
         press_u = press_v = total_u = total_v = jnp.zeros((size_c, size_r), F32)
         deep_u = deep_v = press_u
         for l in range(layers):
-            h = source[H, l]
-            u = source[U, l]
-            v = source[V, l]
+            h = lay[H, l]
+            u = lay[U, l]
+            v = lay[V, l]
             if final:
                 diff_u = rolled(h[:, :rows], -1, 0) - h[:, :rows]
                 diff_v = rolled(h[:cells], -1, 1) - h[:cells]
@@ -492,7 +435,7 @@
                 flux_v = v[:cells] * hv
                 out_u = (flux_u - rolled(flux_u, 1, 0))[:cells]
                 out_v = (flux_v - rolled(flux_v, 1, 1))[:, :rows]
-                results[0, l] = h[:cells, :rows] - FLUX_STEP * (out_u + out_v)
+                h_new[l] = h[:cells, :rows] - FLUX_STEP * (out_u + out_v)
                 diff_u, hu = diff_u[:cells], hu[:cells]
                 diff_v, hv = diff_v[:, :rows], hv[:, :rows]
                 u, v = u[:cells, :rows], v[:cells, :rows]
@@ -508,8 +451,9 @@
             press_v = press_v + diff_v
             ut = u - PRESS_COEF * press_u
             vt = v - PRESS_COEF * press_v
-            trial[0, l, :size_c, :size_r] = ut
-            trial[1, l, :size_c, :size_r] = vt
+            stage = trial if final else halo_trial
+            stage[0, l] = ut
+            stage[1, l] = vt
             total_u = total_u + hu * ut
             total_v = total_v + hv * vt
             if outer == 0:
@@ -519,18 +463,55 @@
             depth[0] = deep_u
             depth[1] = deep_v
         if final:
-            stores[3].start()
+            break
         for k, total in ((U, total_u), (V, total_v)):
-            fix = (means[outer, k - 1, :size_c, :size_r] - total) / depth[k - 1, :size_c, :size_r]
-            open_face = faces[k - 1, :size_c, :size_r] != 0.0
+            fix = (depth[k + 1] - total) / depth[k - 1]
+            open_face = trimmed(base[k - 1]) != 0.0
             for l in range(layers):
-                new = jnp.where(open_face, trial[k - 1, l, :size_c, :size_r] + fix, 0.0)
-                if final:
-                    results[k, l] = new
-                else:
-                    lay[k, l] = new
-            if final:
-                stores[3 + k].start()
+                lay[k, l] = jnp.where(open_face, halo_trial[k - 1, l] + fix, 0.0)
+    fixes[0] = total_u
+    fixes[1] = total_v
+    for cp in second_copies:
+        cp.wait()
+    base[4:7, cells: cells + 8] = late_east[...]
+    base[4:7, cells + 8:] = late_west[...]
+
+    def last_substep(k, sums):
+        sum_u, sum_v = substep_own(k)
+        return sums[0] + sum_u, sums[1] + sum_v
+
+    own = jnp.zeros((cells, rows), F32)
+    sum_u, sum_v = lax.fori_loop(0, NSUB, last_substep, (own, own))
+    for k, total in ((0, sum_u), (1, sum_v)):
+        fixes[k] = (total * (1.0 / NSUB) - fixes[k]) / depth[k, :cells, :rows]
+        faces_out[k] = base[k, :cells, :rows]
+    for k in range(3):
+        state_out[k] = base[4 + k, :cells, :rows]
+
+
+def finish(
+    h_new, trial, fixes, faces, state, eta_out, bu_out, bv_out, h_out, u_out, v_out, results, done,
+):
+    layers = h_out.shape[0]
+    stores = [
+        pltpu.make_async_copy(src, out, done.at[k])
+        for k, (src, out) in enumerate((
+            (h_new, h_out),
+            (state.at[0], eta_out),
+            (state.at[1], bu_out),
+            (state.at[2], bv_out),
+            (results.at[0], u_out),
+            (results.at[1], v_out),
+        ))
+    ]
+    for cp in stores[:4]:
+        cp.start()
+    for k in range(2):
+        open_face = faces[k] != 0.0
+        fix = fixes[k]
+        for l in range(layers):
+            results[k, l] = jnp.where(open_face, trial[k, l] + fix, 0.0)
+        stores[4 + k].start()
     for cp in stores:
         cp.wait()
 
@@ -554,19 +535,22 @@
     mid = pl.pallas_call(
         functools.partial(exchange, devices),
         out_shape=[
-            inner(3, layers, ext, wide), inner(STEPS, 2, ext, wide), inner(2, ext, wide),
-            inner(3, cells, rows),
+            inner(layers, cells, rows), inner(2, layers, cells, rows), inner(2, cells, rows),
+            inner(2, cells, rows), inner(3, cells, rows),
         ],
         in_specs=[anywhere] * 10,
-        out_specs=[vmem] * 4,
+        out_specs=[vmem] * 5,
         scratch_shapes=[
-            inner(7, cells + 24, wide),
+            inner(7, cells + 16, wide),
+            inner(3, layers, ext, wide),
+            inner(2, layers, ext, wide),
+            inner(4, ext, wide),
             pltpu.VMEM(sea_faces.shape, sea_faces.dtype),
             inner(*wind_base.shape),
             pltpu.SMEM(wind_seeds.shape[::-1], wind_seeds.dtype),
             pltpu.SMEM(wind_scale.shape, F32),
             inner(4 * layers, rows), inner(3 * layers, rows), inner(3 * layers, rows), inner(4 * layers, rows),
-            inner(4, 8, rows), inner(4, 8, rows), inner(4, 8, rows), inner(4, 8, rows),
+            inner(3, 8, wide), inner(3, 8, wide),
             inner(cells, 2 * LANES), inner(cells, 2 * LANES), inner(2, cells, LANES), inner(2, cells, LANES),
             inner(cells, 2 * LANES), inner(cells, 2 * LANES), inner(2, cells, LANES), inner(2, cells, LANES),
             pltpu.SemaphoreType.DMA((10,)),
@@ -583,18 +567,12 @@
         sea_faces, wind_base, wind_seeds.T, wind_scale,
     )
     return pl.pallas_call(
-        advance,
+        finish,
         out_shape=[shape(cells, rows)] * 3 + [shape(layers, cells, rows)] * 3,
-        in_specs=[vmem] * 4,
+        in_specs=[vmem] * 5,
         out_specs=[anywhere] * 6,
-        scratch_shapes=[
-            inner(3, layers, ext, wide),
-            inner(2, layers, ext, wide),
-            inner(2, ext, wide),
-            inner(3, layers, cells, rows),
-            pltpu.SemaphoreType.DMA((6,)),
-        ],
-        name="advance",
+        scratch_shapes=[inner(2, layers, cells, rows), pltpu.SemaphoreType.DMA((6,))],
+        name="finish",
     )(*[pltpu.with_memory_space_constraint(x, pltpu.VMEM) for x in mid])
 
 

time: 40 us -> 40.5 us (1.012)
  Pallas kernels: 39.2 us -> 39.7 us
    pallas_call x2, Pallas kernels: 39.2 us -> 39.7 us  [the longest x1 38.6 us: body(): pl.pallas_call(functools.partial(exchange, devices), out_shape=[inner(lay...]
where the time goes in v4:
time: 40.5 us; the launch traced here: 40.4 us
  Pallas kernels  39.7 us (98%)
  between operations  0.64 us (2%)
    pallas_call x1, Pallas kernels, body(): pl.pallas_call(functools.partial(exchange, devices), out_shape=[inner(lay...  38.6 us
    pallas_call x1, Pallas kernels, body(): pl.pallas_call(finish, out_shape=[shape(cells, rows)] * 3 + [shape(layers...  1.16 us

profile of v4, /device:TPU:37, one launch (start us, length us, event | category | flops | bytes accessed | tf_op | source)
XLA Modules:
  0.0 40.4 jit_solution(7877862597182800472)
XLA Ops:
  0.6 38.6 %exchange.1 = (f32[14,16,512]{2,1,0:T(8,128)S(1)}, f32[2,14,16,512]{3,2,1,0:T(8,128)S(1)}, f32[2,16,512]{2,1,0:T(8,128)S(1)}, f32[2,16,512]{2,1,0:T(8,128)S(1)}, f32[3,16,512]{2,1,0:T(8,128)S(1)}) custom-call(f32[16,512]{1,0:T(8,128)} %eta_ref.1, f32[16,512]{1,0:T(8,128)} %bu_ref.1, f32[16,512]{1,0:T(8,128)} %bv_ref.1, f32[14,16,512]{2,1,0:T(8,128)} %h_ref.1, ...), custom_call_target="tpu_custom_call" | custom-call | tf_op jit(solution)/shard_map/exchange/pallas_call | solution.py:535
  39.2 1.2 %finish.1 = (f32[16,512]{1,0:T(8,128)}, f32[16,512]{1,0:T(8,128)}, f32[16,512]{1,0:T(8,128)}, f32[14,16,512]{2,1,0:T(8,128)}, f32[14,16,512]{2,1,0:T(8,128)}, /*index=5*/f32[14,16,512]{2,1,0:T(8,128)}) custom-call(f32[14,16,512]{2,1,0:T(8,128)S(1)} %get-tuple-element.11.h_new, f32[2,14,16,512]{3,2,1,0:T(8,128)S(1)} %get-tuple-element.12.trial, ...), custom_call_target="tpu_custom_call" | custom-call | tf_op jit(solution)/shard_map/finish/pallas_call | solution.py:569

commit v5 on v4

--- a/solution.py
+++ b/solution.py
@@ -190,16 +190,25 @@
         cp.wait()
     last = cells - 1
     h_last = lay[H, :, last, :rows]
-    u_last = lay[U, :, last, :rows]
+    v_last = lay[V, :, last, :rows]
     flux_in = lay[U, :, last - 1, :rows] * (0.5 * (lay[H, :, last - 1, :rows] + h_last))
-    for k, x in enumerate((h_last, u_last, flux_in, lay[V, :, last, :rows])):
+    inside = lane_iota((layers, rows)) < rows - 1
+    along = jnp.where(inside, v_last * (0.5 * (h_last + rolled(h_last, -1, 1))), 0.0)
+    for k, x in enumerate((h_last, lay[U, :, last, :rows], flux_in - (along - rolled(along, 1, 1)))):
         goeast[k * layers: (k + 1) * layers] = x
+    ends = v_last[:, rows - LANES:]
+    spare = 48 - 3 * layers
+    for k in range(0, layers, spare):
+        part = ends[k: k + spare]
+        at = k // spare * LANES
+        goeast[3 * layers: 3 * layers + part.shape[0], at: at + LANES] = part
     h_first = lay[H, :, 0, :rows]
     flux_out = lay[U, :, 0, :rows] * (0.5 * (h_first + lay[H, :, 1, :rows]))
     for k, x in enumerate((h_first, flux_out, lay[V, :, 0, :rows])):
         gowest[k * layers: (k + 1) * layers] = x
 
     side_copies[0].start()
+    strip_rows = ((H, 0), (H, 1), (V, 0), (V, 1), (U, 0))
     lane = lane_iota((cells, LANES))
     hi = rows - LANES
     base_t = jnp.zeros((cells, LANES), F32)
@@ -210,16 +219,15 @@
         base_b = jnp.where(here, rolled(base[f, :cells, :LANES], f * STRIP, 1), base_b)
     lay_t = jnp.zeros((cells, LANES), F32)
     lay_b = jnp.zeros((cells, LANES), F32)
-    for start, width, kind in ((0, 2, H), (2 * layers, 2, V), (4 * layers, 1, U)):
+    for row, (kind, depth_in) in enumerate(strip_rows):
         for l in range(layers):
-            spot = start + width * l
-            here = jnp.logical_and(lane >= spot, lane < spot + width)
-            lay_t = jnp.where(here, rolled(lay[kind, l, :cells, hi:rows], spot + width, 1), lay_t)
-            lay_b = jnp.where(here, rolled(lay[kind, l, :cells, :LANES], spot, 1), lay_b)
+            spot = row * layers + l
+            here = lane == spot
+            lay_t = jnp.where(here, rolled(lay[kind, l, :cells, hi:rows], spot + 1 + depth_in, 1), lay_t)
+            lay_b = jnp.where(here, rolled(lay[kind, l, :cells, :LANES], spot - depth_in, 1), lay_b)
     r2 = lax.broadcasted_iota(jnp.int32, (LANES, LANES), 0)
     c2 = lax.broadcasted_iota(jnp.int32, (LANES, LANES), 1)
     perm_b = jnp.where(r2 == (c2 ^ (STRIP - 1)), 1.0, 0.0).astype(F32)
-    perm_l = jnp.where(r2 == jnp.where(c2 < 4 * layers, c2 ^ 1, c2), 1.0, 0.0).astype(F32)
     r1 = lax.broadcasted_iota(jnp.int32, (cells, cells), 0)
     c1 = lax.broadcasted_iota(jnp.int32, (cells, cells), 1)
     mirror = jnp.where(r1 + c1 == cells - 1, 1.0, 0.0).astype(F32)
@@ -228,15 +236,19 @@
     )
     north_edge = c == 1
     base_t = jnp.where(north_edge, dot(mirror, dot(base_t, perm_b)), base_t)
-    lay_t = jnp.where(north_edge, dot(mirror, dot(lay_t, perm_l)), lay_t)
+    lay_t = jnp.where(north_edge, dot(mirror, lay_t), lay_t)
     sub = lax.broadcasted_iota(jnp.int32, (8, LANES), 0)
+    spare_lane = lane_iota((8, LANES)) >= 7 * STRIP
     for whole, side, fields, columns in ((top, top_side, base_t, lay_t), (bottom, bottom_side, base_b, lay_b)):
         whole[:, :LANES] = fields
         whole[:, LANES:] = columns
-        side[0, 0:8] = jnp.where(sub < 2, pltpu.roll(columns[8:], 2, 0), fields[:8])
-        side[0, 8:16] = fields[8:]
-        side[1, 0:8] = fields[:8]
-        side[1, 8:16] = jnp.where(sub >= 6, pltpu.roll(columns[:8], 6, 0), fields[8:])
+        for k, rows8, first_row in ((0, slice(8, 16), 1), (1, slice(0, 8), 0)):
+            h8, v8, u8 = (
+                rolled(rolled(columns[rows8], 7 * STRIP - row * layers, 1), first_row + j, 0)
+                for j, row in enumerate((0, 2, 4))
+            )
+            spares = jnp.where(sub == 0, h8, jnp.where(sub == 1, v8, u8))
+            side[k] = jnp.where(spare_lane, spares, fields[rows8])
 
     def strips(whole, side, into, into_side, k, own, to_west_slot, to_east_slot, merid):
         return [
@@ -296,11 +308,11 @@
     def _():
         down_copies[2].start()
 
+    @pl.when(jnp.logical_not(late))
+    def _():
+        send_far()
+
     column_copies[1].start()
-
-    @pl.when(jnp.logical_not(late))
-    def _():
-        send_far()
 
     @pl.when(c == 0)
     def _():
@@ -348,7 +360,7 @@
     souths = [south_ref[:, :LANES], south_side[1], south_side[0]]
 
     def ring(x):
-        return (x[OWN][:8], x[OWN][8:], x[EAST][:8], x[WEST][8:])
+        return (x[OWN][:8], x[OWN][8:], x[EAST], x[WEST])
 
     for k, (n, s) in enumerate(zip(ring(norths), ring(souths))):
         for f in range(7):
@@ -389,21 +401,34 @@
     depth[2] = mean_u * (1.0 / NSUB)
     depth[3] = mean_v * (1.0 / NSUB)
 
+    lane8 = lane_iota((8, LANES))
+
     def around(own, sides):
-        halo = jnp.where(far_rows, pltpu.roll(sides[1, 8:], 2, 0), pltpu.roll(sides[0, :8], 6, 0))
+        def unpacked(x, row):
+            h8, v8, u8 = (
+                rolled(rolled(x, r * layers - 7 * STRIP, 1), row - j, 0) for j, r in enumerate((0, 2, 4))
+            )
+            return jnp.where(lane8 < layers, h8, jnp.where(lane8 < 4 * layers, v8, u8))
+
+        halo = jnp.where(far_rows, unpacked(sides[1], 0), unpacked(sides[0], 7))
         return jnp.concatenate([own[:, LANES:], halo], 0)
 
     north = around(north_ref, north_side)
     south = around(south_ref, south_side)
-    first24 = lane_iota(north.shape) < LANES // 2
-    for kind, start, width in ((H, 0, 2), (U, 4 * layers, 1), (V, 2 * layers, 2)):
+    lane24 = lane_iota(north.shape)
+    first24 = lane24 < LANES // 2
+    for kind, row, deep_row in ((H, 0, True), (U, 4, False), (V, 2, True)):
         for l in range(layers):
-            spot = start + width * l
-            lay[kind, l, :, rows:] = jnp.where(
-                first24, rolled(north, -spot, 1), rolled(south, LANES - width - spot, 1)
-            )
+            spot = row * layers + l
+            n = rolled(north, -spot, 1)
+            s = rolled(south, LANES - 1 - spot, 1)
+            if deep_row:
+                n = jnp.where(lane24 == 0, n, rolled(north, 1 - spot - layers, 1))
+                s = jnp.where(lane24 == LANES - 1, s, rolled(south, LANES - 2 - spot - layers, 1))
+            lay[kind, l, :, rows:] = jnp.where(first24, n, s)
     for cp in column_copies:
         cp.wait()
+    end_lane = lane_iota((1, LANES)) == LANES - 1
     for l in range(layers):
         def column(ref, k):
             return ref[k * layers + l: k * layers + l + 1, :]
@@ -416,7 +441,10 @@
         lay[H, l, ext - 2: ext - 1, :rows] = 2.0 - column(lwest, 0)
         lay[U, l, ext - 1: ext, :rows] = column(lwest, 1)
         lay[U, l, ext - 2: ext - 1, :rows] = column(lwest, 2)
-        lay[V, l, ext - 1: ext, :rows] = column(lwest, 3)
+        at = l // spare * LANES
+        lay[V, l, ext - 1: ext, rows - LANES: rows] = jnp.where(
+            end_lane, lwest[3 * layers + l % spare: 3 * layers + l % spare + 1, at: at + LANES], 0.0
+        )
     for outer in range(STEPS):
         final = outer == STEPS - 1
         size_c, size_r = (cells, rows) if final else (ext, wide)
@@ -549,10 +577,10 @@
             inner(*wind_base.shape),
             pltpu.SMEM(wind_seeds.shape[::-1], wind_seeds.dtype),
             pltpu.SMEM(wind_scale.shape, F32),
-            inner(4 * layers, rows), inner(3 * layers, rows), inner(3 * layers, rows), inner(4 * layers, rows),
+            inner(48, rows), inner(3 * layers, rows), inner(3 * layers, rows), inner(48, rows),
             inner(3, 8, wide), inner(3, 8, wide),
-            inner(cells, 2 * LANES), inner(cells, 2 * LANES), inner(2, cells, LANES), inner(2, cells, LANES),
-            inner(cells, 2 * LANES), inner(cells, 2 * LANES), inner(2, cells, LANES), inner(2, cells, LANES),
+            inner(cells, 2 * LANES), inner(cells, 2 * LANES), inner(2, 8, LANES), inner(2, 8, LANES),
+            inner(cells, 2 * LANES), inner(cells, 2 * LANES), inner(2, 8, LANES), inner(2, 8, LANES),
             pltpu.SemaphoreType.DMA((10,)),
             pltpu.SemaphoreType.DMA((17,)),
             pltpu.SemaphoreType.DMA((17,)),

time: 40.5 us -> 38.8 us (0.958)
  Pallas kernels: 39.7 us -> 38.1 us
    pallas_call x1, Pallas kernels: 38.6 us -> 36.9 us  [body(): pl.pallas_call(functools.partial(exchange, devices), out_shape=[inner(lay...]
where the time goes in v5:
time: 38.8 us; the launch traced here: 38.7 us
  Pallas kernels  38.1 us (98%)
  between operations  0.64 us (2%)
    pallas_call x1, Pallas kernels, body(): pl.pallas_call(functools.partial(exchange, devices), out_shape=[inner(lay...  36.9 us
    pallas_call x1, Pallas kernels, body(): pl.pallas_call(finish, out_shape=[shape(cells, rows)] * 3 + [shape(layers...  1.16 us

profile of v5, /device:TPU:37, one launch (start us, length us, event | category | flops | bytes accessed | tf_op | source)
XLA Modules:
  0.0 38.7 jit_solution(14867421556887204286)
XLA Ops:
  0.6 36.9 %exchange.1 = (f32[14,16,512]{2,1,0:T(8,128)S(1)}, f32[2,14,16,512]{3,2,1,0:T(8,128)S(1)}, f32[2,16,512]{2,1,0:T(8,128)S(1)}, f32[2,16,512]{2,1,0:T(8,128)S(1)}, f32[3,16,512]{2,1,0:T(8,128)S(1)}) custom-call(f32[16,512]{1,0:T(8,128)} %eta_ref.1, f32[16,512]{1,0:T(8,128)} %bu_ref.1, f32[16,512]{1,0:T(8,128)} %bv_ref.1, f32[14,16,512]{2,1,0:T(8,128)} %h_ref.1, ...), custom_call_target="tpu_custom_call" | custom-call | tf_op jit(solution)/shard_map/exchange/pallas_call | solution.py:563
  37.6 1.2 %finish.1 = (f32[16,512]{1,0:T(8,128)}, f32[16,512]{1,0:T(8,128)}, f32[16,512]{1,0:T(8,128)}, f32[14,16,512]{2,1,0:T(8,128)}, f32[14,16,512]{2,1,0:T(8,128)}, /*index=5*/f32[14,16,512]{2,1,0:T(8,128)}) custom-call(f32[14,16,512]{2,1,0:T(8,128)S(1)} %get-tuple-element.11.h_new, f32[2,14,16,512]{3,2,1,0:T(8,128)S(1)} %get-tuple-element.12.trial, ...), custom_call_target="tpu_custom_call" | custom-call | tf_op jit(solution)/shard_map/finish/pallas_call | solution.py:597

commit v6 on v5

--- a/solution.py
+++ b/solution.py
@@ -62,7 +62,7 @@
     devices,
     eta_ref, bu_ref, bv_ref, h_ref, u_ref, v_ref, faces_ref, base_ref, seeds_ref, scale_ref,
     h_new, trial, fixes, faces_out, state_out,
-    base, lay, halo_trial, depth, faces, winds, seeds, scale, goeast, gowest, least, lwest, late_east, late_west,
+    base, lay, trial_u, trial_v, leaving, depth, faces, winds, seeds, scale, goeast, gowest, least, lwest, late_east, late_west,
     top, bottom, top_side, bottom_side, north_ref, south_ref, north_side, south_side,
     load, send, recv, near_ok, west_ok, far_ok,
 ):
@@ -137,9 +137,6 @@
         copy(gowest, least, 14, w, c),
     ]
 
-    for cp in fetches[:3]:
-        cp.wait()
-
     def tell(semaphore, zonal, merid):
         pl.semaphore_signal(
             semaphore, inc=1, device_id={"zonal": zonal, "merid": merid}, device_id_type=MESH
@@ -156,6 +153,8 @@
     def _():
         pl.semaphore_wait(near_ok, 1)
 
+    for cp in fetches[:3]:
+        cp.wait()
     state_copies[0].start()
     for cp in fetches[3:7]:
         cp.wait()
@@ -188,25 +187,6 @@
     base[1, :cells, :rows] = mask_v * wave
     for cp in fetches[8:]:
         cp.wait()
-    last = cells - 1
-    h_last = lay[H, :, last, :rows]
-    v_last = lay[V, :, last, :rows]
-    flux_in = lay[U, :, last - 1, :rows] * (0.5 * (lay[H, :, last - 1, :rows] + h_last))
-    inside = lane_iota((layers, rows)) < rows - 1
-    along = jnp.where(inside, v_last * (0.5 * (h_last + rolled(h_last, -1, 1))), 0.0)
-    for k, x in enumerate((h_last, lay[U, :, last, :rows], flux_in - (along - rolled(along, 1, 1)))):
-        goeast[k * layers: (k + 1) * layers] = x
-    ends = v_last[:, rows - LANES:]
-    spare = 48 - 3 * layers
-    for k in range(0, layers, spare):
-        part = ends[k: k + spare]
-        at = k // spare * LANES
-        goeast[3 * layers: 3 * layers + part.shape[0], at: at + LANES] = part
-    h_first = lay[H, :, 0, :rows]
-    flux_out = lay[U, :, 0, :rows] * (0.5 * (h_first + lay[H, :, 1, :rows]))
-    for k, x in enumerate((h_first, flux_out, lay[V, :, 0, :rows])):
-        gowest[k * layers: (k + 1) * layers] = x
-
     side_copies[0].start()
     strip_rows = ((H, 0), (H, 1), (V, 0), (V, 1), (U, 0))
     lane = lane_iota((cells, LANES))
@@ -294,6 +274,25 @@
     def _():
         send_far()
 
+    last = cells - 1
+    h_last = lay[H, :, last, :rows]
+    v_last = lay[V, :, last, :rows]
+    flux_in = lay[U, :, last - 1, :rows] * (0.5 * (lay[H, :, last - 1, :rows] + h_last))
+    inside = lane_iota((layers, rows)) < rows - 1
+    along = jnp.where(inside, v_last * (0.5 * (h_last + rolled(h_last, -1, 1))), 0.0)
+    for k, x in enumerate((h_last, lay[U, :, last, :rows], flux_in - (along - rolled(along, 1, 1)))):
+        goeast[k * layers: (k + 1) * layers] = x
+    ends = v_last[:, rows - LANES:]
+    spare = 48 - 3 * layers
+    for k in range(0, layers, spare):
+        part = ends[k: k + spare]
+        at = k // spare * LANES
+        goeast[3 * layers: 3 * layers + part.shape[0], at: at + LANES] = part
+    h_first = lay[H, :, 0, :rows]
+    flux_out = lay[U, :, 0, :rows] * (0.5 * (h_first + lay[H, :, 1, :rows]))
+    for k, x in enumerate((h_first, flux_out, lay[V, :, 0, :rows])):
+        gowest[k * layers: (k + 1) * layers] = x
+
     column_copies[0].start()
 
     pl.semaphore_wait(west_ok, 1)
@@ -373,29 +372,33 @@
     def trimmed(x):
         return jnp.concatenate([x[:cells], jnp.where(near, x[cells: cells + 8], x[cells + 8:])], 0)
 
-    def move(_):
+    def move(first=False):
         bu = base[5]
         bv = base[6]
         eta = base[4] - (bu - at_west(bu) + bv - at_south(bv))
         base[4] = eta
         au = base[0]
-        bu = jnp.where(au != 0.0, bu - au * (at_east(eta) - eta) + base[2], 0.0)
+        bu = bu - au * (at_east(eta) - eta) + base[2]
+        if first:
+            bu = jnp.where(au != 0.0, bu, 0.0)
         base[5] = bu
         av = base[1]
-        bv = jnp.where(av != 0.0, bv - av * (at_north(eta) - eta) + base[3], 0.0)
+        bv = bv - av * (at_north(eta) - eta) + base[3]
+        if first:
+            bv = jnp.where(av != 0.0, bv, 0.0)
         base[6] = bv
         return bu, bv
 
-    def substep(k, sums):
-        bu, bv = move(k)
+    def substep(_, sums):
+        bu, bv = move()
         return sums[0] + trimmed(bu), sums[1] + trimmed(bv)
 
-    def substep_own(k):
-        bu, bv = move(k)
+    def substep_own():
+        bu, bv = move()
         return bu[:cells, :rows], bv[:cells, :rows]
 
-    zero = jnp.zeros((ext, wide), F32)
-    mean_u, mean_v = lax.fori_loop(0, NSUB, substep, (zero, zero))
+    first_u, first_v = move(first=True)
+    mean_u, mean_v = lax.fori_loop(1, NSUB, substep, (trimmed(first_u), trimmed(first_v)))
     for cp in second_copies:
         cp.start()
     depth[2] = mean_u * (1.0 / NSUB)
@@ -426,6 +429,24 @@
                 n = jnp.where(lane24 == 0, n, rolled(north, 1 - spot - layers, 1))
                 s = jnp.where(lane24 == LANES - 1, s, rolled(south, LANES - 2 - spot - layers, 1))
             lay[kind, l, :, rows:] = jnp.where(first24, n, s)
+    press = total = deep = jnp.zeros((cells, wide), F32)
+    for l in range(layers):
+        h = lay[H, l, :cells]
+        v = lay[V, l, :cells]
+        diff = at_north(h) - h
+        press = press + diff
+        half = h + 0.5 * diff
+        flux = v * half
+        leaving[l] = flux - at_south(flux)
+        vt = v - PRESS_COEF * press
+        trial_v[l] = vt
+        total = total + half * vt
+        deep = deep + half
+    depth[1, :cells] = deep
+    fix = (depth[3, :cells] - total) / deep
+    open_face = base[1, :cells] != 0.0
+    for l in range(layers):
+        lay[V, l, :cells] = jnp.where(open_face, trial_v[l] + fix, 0.0)
     for cp in column_copies:
         cp.wait()
     end_lane = lane_iota((1, LANES)) == LANES - 1
@@ -445,58 +466,50 @@
         lay[V, l, ext - 1: ext, rows - LANES: rows] = jnp.where(
             end_lane, lwest[3 * layers + l % spare: 3 * layers + l % spare + 1, at: at + LANES], 0.0
         )
-    for outer in range(STEPS):
-        final = outer == STEPS - 1
-        size_c, size_r = (cells, rows) if final else (ext, wide)
-        press_u = press_v = total_u = total_v = jnp.zeros((size_c, size_r), F32)
-        deep_u = deep_v = press_u
-        for l in range(layers):
-            h = lay[H, l]
-            u = lay[U, l]
-            v = lay[V, l]
-            if final:
-                diff_u = rolled(h[:, :rows], -1, 0) - h[:, :rows]
-                diff_v = rolled(h[:cells], -1, 1) - h[:cells]
-                hu = h[:, :rows] + 0.5 * diff_u
-                hv = h[:cells] + 0.5 * diff_v
-                flux_u = u[:, :rows] * hu
-                flux_v = v[:cells] * hv
-                out_u = (flux_u - rolled(flux_u, 1, 0))[:cells]
-                out_v = (flux_v - rolled(flux_v, 1, 1))[:, :rows]
-                h_new[l] = h[:cells, :rows] - FLUX_STEP * (out_u + out_v)
-                diff_u, hu = diff_u[:cells], hu[:cells]
-                diff_v, hv = diff_v[:, :rows], hv[:, :rows]
-                u, v = u[:cells, :rows], v[:cells, :rows]
-            else:
-                diff_u = at_east(h) - h
-                diff_v = at_north(h) - h
-                hu = h + 0.5 * diff_u
-                hv = h + 0.5 * diff_v
-                flux_u = u * hu
-                flux_v = v * hv
-                lay[H, l] = h - FLUX_STEP * (flux_u - at_west(flux_u) + flux_v - at_south(flux_v))
-            press_u = press_u + diff_u
-            press_v = press_v + diff_v
-            ut = u - PRESS_COEF * press_u
-            vt = v - PRESS_COEF * press_v
-            stage = trial if final else halo_trial
-            stage[0, l] = ut
-            stage[1, l] = vt
-            total_u = total_u + hu * ut
-            total_v = total_v + hv * vt
-            if outer == 0:
-                deep_u = deep_u + hu
-                deep_v = deep_v + hv
-        if outer == 0:
-            depth[0] = deep_u
-            depth[1] = deep_v
-        if final:
-            break
-        for k, total in ((U, total_u), (V, total_v)):
-            fix = (depth[k + 1] - total) / depth[k - 1]
-            open_face = trimmed(base[k - 1]) != 0.0
-            for l in range(layers):
-                lay[k, l] = jnp.where(open_face, halo_trial[k - 1, l] + fix, 0.0)
+    press = total = deep = jnp.zeros((ext, wide), F32)
+    for l in range(layers):
+        h = lay[H, l]
+        u = lay[U, l]
+        diff = at_east(h) - h
+        press = press + diff
+        half = h + 0.5 * diff
+        flux = u * half
+        side_h = h[cells:]
+        side_flux = lay[V, l, cells:] * (side_h + 0.5 * (at_north(side_h) - side_h))
+        out_v = jnp.concatenate([leaving[l], side_flux - at_south(side_flux)], 0)
+        lay[H, l] = h - FLUX_STEP * (flux - at_west(flux) + out_v)
+        ut = u - PRESS_COEF * press
+        trial_u[l] = ut[:, :rows]
+        total = total + half * ut
+        deep = deep + half
+    depth[0] = deep
+    fix = ((depth[2] - total) / deep)[:, :rows]
+    open_face = trimmed(base[0])[:, :rows] != 0.0
+    for l in range(layers):
+        lay[U, l, :, :rows] = jnp.where(open_face, trial_u[l] + fix, 0.0)
+    press_u = press_v = total_u = total_v = jnp.zeros((cells, rows), F32)
+    for l in range(layers):
+        h_u = lay[H, l, :, :rows]
+        h_v = lay[H, l, :cells]
+        diff_u = rolled(h_u, -1, 0) - h_u
+        diff_v = rolled(h_v, -1, 1) - h_v
+        hu = h_u + 0.5 * diff_u
+        hv = h_v + 0.5 * diff_v
+        u = lay[U, l, :, :rows]
+        v = lay[V, l, :cells]
+        flux_u = u * hu
+        flux_v = v * hv
+        out_u = (flux_u - rolled(flux_u, 1, 0))[:cells]
+        out_v = (flux_v - rolled(flux_v, 1, 1))[:, :rows]
+        h_new[l] = h_u[:cells] - FLUX_STEP * (out_u + out_v)
+        press_u = press_u + diff_u[:cells]
+        press_v = press_v + diff_v[:, :rows]
+        ut = u[:cells] - PRESS_COEF * press_u
+        vt = v[:, :rows] - PRESS_COEF * press_v
+        trial[0, l] = ut
+        trial[1, l] = vt
+        total_u = total_u + hu[:cells] * ut
+        total_v = total_v + hv[:, :rows] * vt
     fixes[0] = total_u
     fixes[1] = total_v
     for cp in second_copies:
@@ -505,7 +518,7 @@
     base[4:7, cells + 8:] = late_west[...]
 
     def last_substep(k, sums):
-        sum_u, sum_v = substep_own(k)
+        sum_u, sum_v = substep_own()
         return sums[0] + sum_u, sums[1] + sum_v
 
     own = jnp.zeros((cells, rows), F32)
@@ -528,9 +541,14 @@
             (state.at[0], eta_out),
             (state.at[1], bu_out),
             (state.at[2], bv_out),
-            (results.at[0], u_out),
-            (results.at[1], v_out),
         ))
+    ]
+    half = layers // 2
+    parts = (pl.ds(0, half), pl.ds(half, layers - half))
+    stores += [
+        pltpu.make_async_copy(results.at[k, part], out.at[part], done.at[4 + 2 * k + j])
+        for k, out in enumerate((u_out, v_out))
+        for j, part in enumerate(parts)
     ]
     for cp in stores[:4]:
         cp.start()
@@ -539,7 +557,9 @@
         fix = fixes[k]
         for l in range(layers):
             results[k, l] = jnp.where(open_face, trial[k, l] + fix, 0.0)
-        stores[4 + k].start()
+            if l == half - 1:
+                stores[4 + 2 * k].start()
+        stores[5 + 2 * k].start()
     for cp in stores:
         cp.wait()
 
@@ -571,7 +591,9 @@
         scratch_shapes=[
             inner(7, cells + 16, wide),
             inner(3, layers, ext, wide),
-            inner(2, layers, ext, wide),
+            inner(layers, ext, rows),
+            inner(layers, cells, wide),
+            inner(layers, cells, wide),
             inner(4, ext, wide),
             pltpu.VMEM(sea_faces.shape, sea_faces.dtype),
             inner(*wind_base.shape),
@@ -599,7 +621,7 @@
         out_shape=[shape(cells, rows)] * 3 + [shape(layers, cells, rows)] * 3,
         in_specs=[vmem] * 5,
         out_specs=[anywhere] * 6,
-        scratch_shapes=[inner(2, layers, cells, rows), pltpu.SemaphoreType.DMA((6,))],
+        scratch_shapes=[inner(2, layers, cells, rows), pltpu.SemaphoreType.DMA((8,))],
         name="finish",
     )(*[pltpu.with_memory_space_constraint(x, pltpu.VMEM) for x in mid])
 

time: 38.8 us -> 38.6 us (level)
  no operation moved by 1% of the time
where the time goes in v6:
time: 38.6 us; the launch traced here: 38.5 us
  Pallas kernels  37.9 us (98%)
  between operations  0.64 us (2%)
    pallas_call x1, Pallas kernels, body(): pl.pallas_call(functools.partial(exchange, devices), out_shape=[inner(lay...  36.7 us
    pallas_call x1, Pallas kernels, body(): pl.pallas_call(finish, out_shape=[shape(cells, rows)] * 3 + [shape(layers...  1.17 us

profile of v6, /device:TPU:37, one launch (start us, length us, event | category | flops | bytes accessed | tf_op | source)
XLA Modules:
  0.0 38.5 jit_solution(5296619312108075285)
XLA Ops:
  0.6 36.7 %exchange.1 = (f32[14,16,512]{2,1,0:T(8,128)S(1)}, f32[2,14,16,512]{3,2,1,0:T(8,128)S(1)}, f32[2,16,512]{2,1,0:T(8,128)S(1)}, f32[2,16,512]{2,1,0:T(8,128)S(1)}, f32[3,16,512]{2,1,0:T(8,128)S(1)}) custom-call(f32[16,512]{1,0:T(8,128)} %eta_ref.1, f32[16,512]{1,0:T(8,128)} %bu_ref.1, f32[16,512]{1,0:T(8,128)} %bv_ref.1, f32[14,16,512]{2,1,0:T(8,128)} %h_ref.1, ...), custom_call_target="tpu_custom_call" | custom-call | tf_op jit(solution)/shard_map/exchange/pallas_call | solution.py:583
  37.3 1.2 %finish.1 = (f32[16,512]{1,0:T(8,128)}, f32[16,512]{1,0:T(8,128)}, f32[16,512]{1,0:T(8,128)}, f32[14,16,512]{2,1,0:T(8,128)}, f32[14,16,512]{2,1,0:T(8,128)}, /*index=5*/f32[14,16,512]{2,1,0:T(8,128)}) custom-call(f32[14,16,512]{2,1,0:T(8,128)S(1)} %get-tuple-element.11.h_new, f32[2,14,16,512]{3,2,1,0:T(8,128)S(1)} %get-tuple-element.12.trial, ...), custom_call_target="tpu_custom_call" | custom-call | tf_op jit(solution)/shard_map/finish/pallas_call | solution.py:619

commit v7 on v6

--- a/solution.py
+++ b/solution.py
@@ -62,7 +62,7 @@
     devices,
     eta_ref, bu_ref, bv_ref, h_ref, u_ref, v_ref, faces_ref, base_ref, seeds_ref, scale_ref,
     h_new, trial, fixes, faces_out, state_out,
-    base, lay, trial_u, trial_v, leaving, depth, faces, winds, seeds, scale, goeast, gowest, least, lwest, late_east, late_west,
+    base, lay, trial_u, trial_v, leaving, depth, faces, winds, seeds, scale, goeast, gowest, least, lwest, late_east, late_west, late_strips, strips_east, strips_west,
     top, bottom, top_side, bottom_side, north_ref, south_ref, north_side, south_side,
     load, send, recv, near_ok, west_ok, far_ok,
 ):
@@ -129,8 +129,10 @@
     state_copies = to_sides(pl.ds(4, 3), 15)
     side_copies = to_sides(pl.ds(0, 4), 0)
     second_copies = [
-        copy(base.at[pl.ds(4, 3), pl.ds(8, 8)], late_west, 2, e, c),
-        copy(base.at[pl.ds(4, 3), pl.ds(0, 8)], late_east, 3, w, c),
+        copy(base.at[pl.ds(4, 3), pl.ds(8, 8), lanes], late_west, 2, e, c),
+        copy(base.at[pl.ds(4, 3), pl.ds(0, 8), lanes], late_east, 3, w, c),
+        copy(late_strips.at[1], strips_west, 17, e, c),
+        copy(late_strips.at[0], strips_east, 18, w, c),
     ]
     column_copies = [
         copy(goeast, lwest, 13, e, c),
@@ -399,7 +401,15 @@
 
     first_u, first_v = move(first=True)
     mean_u, mean_v = lax.fori_loop(1, NSUB, substep, (trimmed(first_u), trimmed(first_v)))
-    for cp in second_copies:
+    for cp in second_copies[:2]:
+        cp.start()
+    for k in range(2):
+        packed = jnp.zeros((8, LANES), F32)
+        for j in range(3):
+            strip = rolled(base[4 + j, 8 * k: 8 * k + 8, rows:], STRIP + 2 * STRIP * j, 1)
+            packed = jnp.where(lane_iota((8, LANES)) // (2 * STRIP) == j, strip, packed)
+        late_strips[k] = packed
+    for cp in second_copies[2:]:
         cp.start()
     depth[2] = mean_u * (1.0 / NSUB)
     depth[3] = mean_v * (1.0 / NSUB)
@@ -514,8 +524,11 @@
     fixes[1] = total_v
     for cp in second_copies:
         cp.wait()
-    base[4:7, cells: cells + 8] = late_east[...]
-    base[4:7, cells + 8:] = late_west[...]
+    base[4:7, cells: cells + 8, :rows] = late_east[...]
+    base[4:7, cells + 8:, :rows] = late_west[...]
+    for j in range(3):
+        base[4 + j, cells: cells + 8, rows:] = rolled(strips_east[...], -STRIP - 2 * STRIP * j, 1)
+        base[4 + j, cells + 8:, rows:] = rolled(strips_west[...], -STRIP - 2 * STRIP * j, 1)
 
     def last_substep(k, sums):
         sum_u, sum_v = substep_own()
@@ -600,12 +613,12 @@
             pltpu.SMEM(wind_seeds.shape[::-1], wind_seeds.dtype),
             pltpu.SMEM(wind_scale.shape, F32),
             inner(48, rows), inner(3 * layers, rows), inner(3 * layers, rows), inner(48, rows),
-            inner(3, 8, wide), inner(3, 8, wide),
+            inner(3, 8, rows), inner(3, 8, rows), inner(2, 8, LANES), inner(8, LANES), inner(8, LANES),
             inner(cells, 2 * LANES), inner(cells, 2 * LANES), inner(2, 8, LANES), inner(2, 8, LANES),
             inner(cells, 2 * LANES), inner(cells, 2 * LANES), inner(2, 8, LANES), inner(2, 8, LANES),
             pltpu.SemaphoreType.DMA((10,)),
-            pltpu.SemaphoreType.DMA((17,)),
-            pltpu.SemaphoreType.DMA((17,)),
+            pltpu.SemaphoreType.DMA((19,)),
+            pltpu.SemaphoreType.DMA((19,)),
             pltpu.SemaphoreType.REGULAR,
             pltpu.SemaphoreType.REGULAR,
             pltpu.SemaphoreType.REGULAR,

time: 38.6 us -> 38.4 us (level)
  no operation moved by 1% of the time
where the time goes in v7:
time: 38.4 us; the launch traced here: 38.3 us
  Pallas kernels  37.6 us (98%)
  between operations  0.64 us (2%)
    pallas_call x1, Pallas kernels, body(): pl.pallas_call(functools.partial(exchange, devices), out_shape=[inner(lay...  36.5 us
    pallas_call x1, Pallas kernels, body(): pl.pallas_call(finish, out_shape=[shape(cells, rows)] * 3 + [shape(layers...  1.17 us

profile of v7, /device:TPU:37, one launch (start us, length us, event | category | flops | bytes accessed | tf_op | source)
XLA Modules:
  0.0 38.3 jit_solution(10449601001013632263)
XLA Ops:
  0.6 36.5 %exchange.1 = (f32[14,16,512]{2,1,0:T(8,128)S(1)}, f32[2,14,16,512]{3,2,1,0:T(8,128)S(1)}, f32[2,16,512]{2,1,0:T(8,128)S(1)}, f32[2,16,512]{2,1,0:T(8,128)S(1)}, f32[3,16,512]{2,1,0:T(8,128)S(1)}) custom-call(f32[16,512]{1,0:T(8,128)} %eta_ref.1, f32[16,512]{1,0:T(8,128)} %bu_ref.1, f32[16,512]{1,0:T(8,128)} %bv_ref.1, f32[14,16,512]{2,1,0:T(8,128)} %h_ref.1, ...), custom_call_target="tpu_custom_call" | custom-call | tf_op jit(solution)/shard_map/exchange/pallas_call | solution.py:596
  37.1 1.2 %finish.1 = (f32[16,512]{1,0:T(8,128)}, f32[16,512]{1,0:T(8,128)}, f32[16,512]{1,0:T(8,128)}, f32[14,16,512]{2,1,0:T(8,128)}, f32[14,16,512]{2,1,0:T(8,128)}, /*index=5*/f32[14,16,512]{2,1,0:T(8,128)}) custom-call(f32[14,16,512]{2,1,0:T(8,128)S(1)} %get-tuple-element.11.h_new, f32[2,14,16,512]{3,2,1,0:T(8,128)S(1)} %get-tuple-element.12.trial, ...), custom_call_target="tpu_custom_call" | custom-call | tf_op jit(solution)/shard_map/finish/pallas_call | solution.py:632

commit v8 on v7

--- a/solution.py
+++ b/solution.py
@@ -439,6 +439,16 @@
                 n = jnp.where(lane24 == 0, n, rolled(north, 1 - spot - layers, 1))
                 s = jnp.where(lane24 == LANES - 1, s, rolled(south, LANES - 2 - spot - layers, 1))
             lay[kind, l, :, rows:] = jnp.where(first24, n, s)
+    column_copies[1].wait_recv()
+    for l in range(layers):
+        def column(ref, k):
+            return ref[k * layers + l: k * layers + l + 1, :]
+
+        lay[H, l, cells: cells + 1, :rows] = column(least, 0)
+        lay[H, l, cells + 1: cells + 2, :rows] = 2.0 - column(least, 0)
+        lay[U, l, cells: cells + 1, :rows] = column(least, 1)
+        lay[V, l, cells: cells + 1, :rows] = column(least, 2)
+
     press = total = deep = jnp.zeros((cells, wide), F32)
     for l in range(layers):
         h = lay[H, l, :cells]
@@ -458,16 +468,13 @@
     for l in range(layers):
         lay[V, l, :cells] = jnp.where(open_face, trial_v[l] + fix, 0.0)
     for cp in column_copies:
-        cp.wait()
+        cp.wait_send()
+    column_copies[0].wait_recv()
     end_lane = lane_iota((1, LANES)) == LANES - 1
     for l in range(layers):
         def column(ref, k):
             return ref[k * layers + l: k * layers + l + 1, :]
 
-        lay[H, l, cells: cells + 1, :rows] = column(least, 0)
-        lay[H, l, cells + 1: cells + 2, :rows] = 2.0 - column(least, 0)
-        lay[U, l, cells: cells + 1, :rows] = column(least, 1)
-        lay[V, l, cells: cells + 1, :rows] = column(least, 2)
         lay[H, l, ext - 1: ext, :rows] = column(lwest, 0)
         lay[H, l, ext - 2: ext - 1, :rows] = 2.0 - column(lwest, 0)
         lay[U, l, ext - 1: ext, :rows] = column(lwest, 1)

time: 38.4 us -> 38.4 us (level)
  no operation moved by 1% of the time
where the time goes in v8:
time: 38.4 us; the launch traced here: 38.2 us
  Pallas kernels  37.6 us (98%)
  between operations  0.64 us (2%)
    pallas_call x1, Pallas kernels, body(): pl.pallas_call(functools.partial(exchange, devices), out_shape=[inner(lay...  36.4 us
    pallas_call x1, Pallas kernels, body(): pl.pallas_call(finish, out_shape=[shape(cells, rows)] * 3 + [shape(layers...  1.17 us

profile of v8, /device:TPU:37, one launch (start us, length us, event | category | flops | bytes accessed | tf_op | source)
XLA Modules:
  0.0 38.2 jit_solution(16297380523013954358)
XLA Ops:
  0.6 36.4 %exchange.1 = (f32[14,16,512]{2,1,0:T(8,128)S(1)}, f32[2,14,16,512]{3,2,1,0:T(8,128)S(1)}, f32[2,16,512]{2,1,0:T(8,128)S(1)}, f32[2,16,512]{2,1,0:T(8,128)S(1)}, f32[3,16,512]{2,1,0:T(8,128)S(1)}) custom-call(f32[16,512]{1,0:T(8,128)} %eta_ref.1, f32[16,512]{1,0:T(8,128)} %bu_ref.1, f32[16,512]{1,0:T(8,128)} %bv_ref.1, f32[14,16,512]{2,1,0:T(8,128)} %h_ref.1, ...), custom_call_target="tpu_custom_call" | custom-call | tf_op jit(solution)/shard_map/exchange/pallas_call | solution.py:603
  37.1 1.2 %finish.1 = (f32[16,512]{1,0:T(8,128)}, f32[16,512]{1,0:T(8,128)}, f32[16,512]{1,0:T(8,128)}, f32[14,16,512]{2,1,0:T(8,128)}, f32[14,16,512]{2,1,0:T(8,128)}, /*index=5*/f32[14,16,512]{2,1,0:T(8,128)}) custom-call(f32[14,16,512]{2,1,0:T(8,128)S(1)} %get-tuple-element.11.h_new, f32[2,14,16,512]{3,2,1,0:T(8,128)S(1)} %get-tuple-element.12.trial, ...), custom_call_target="tpu_custom_call" | custom-call | tf_op jit(solution)/shard_map/finish/pallas_call | solution.py:639
